TPU v7x, 32 devices: a whole 2x2x4 slice. The times are simulated.
32 devices in a mesh: rep: 1, r: 4 (over z), s: 8 (over x, y, core).
Axes of the slice: x: 2, y: 2, z: 4, core: 2. Of those that a mesh axis runs over, the one named last changes fastest.
Arguments:
- x: bfloat16 [32, 4096, 768], P(('rep', 'r', 's'))
- dy: bfloat16 [32, 4096, 768], P(('rep', 'r', 's'))
- w_gate: bfloat16 [2, 768, 2048], P(None, 's')
- w_up: bfloat16 [2, 768, 2048], P(None, 's')
- w_down: bfloat16 [2, 2048, 768], P(None, 's')
Outputs:
- output 1: bfloat16 [32, 4096, 768], P(('rep', 'r', 's'))
- output 2: bfloat16 [2, 768, 2048], P('rep', 's')
- output 3: bfloat16 [2, 768, 2048], P('rep', 's')
- output 4: bfloat16 [2, 2048, 768], P('rep', 's')
All inputs are finite; a program needn't handle non-finite values.
Results may differ from a plain program's by a relative error of at most 0.018.
Values are sent between devices in bfloat16 or wider.
A program may use at most 2 GiB of HBM per device.

v0:
```python
import jax
import jax.numpy as jnp
from jax import lax
from jax.sharding import PartitionSpec as P

NAMES = ("w_gate", "w_up", "w_down")


def matmul(a, w):
    return jnp.dot(a, w, preferred_element_type=jnp.float32).astype(jnp.bfloat16)


def normed(h):
    wide = h.astype(jnp.float32)
    scale = lax.rsqrt(jnp.mean(wide**2, -1, keepdims=True) + 1e-6)
    return (wide * scale).astype(jnp.bfloat16)


def layer(h, w):
    a = normed(h)
    gate = jnp.dot(a, w["w_gate"], preferred_element_type=jnp.float32)
    up = jnp.dot(a, w["w_up"], preferred_element_type=jnp.float32)
    return h + matmul((jax.nn.silu(gate) * up).astype(jnp.bfloat16), w["w_down"])


def solution(mesh):
    def fetched(weights, number):
        return {name: lax.all_gather(w[number], "s", axis=0, tiled=True) for name, w in zip(NAMES, weights, strict=True)}

    def summed(term):
        return lax.psum(lax.psum_scatter(term, "s", scatter_dimension=0, tiled=True), "r")

    def step(x, dy, *weights):
        layers = weights[0].shape[0]
        h, inputs = x[0], []
        for number in range(layers):
            inputs.append(h)
            h = layer(h, fetched(weights, number))
        by_h, mine = dy[0], [None] * layers
        for number in reversed(range(layers)):
            _, back = jax.vjp(lambda w, h: layer(h, w), fetched(weights, number), inputs[number])
            by_w, by_h = back(by_h)
            mine[number] = [summed(by_w[name]) for name in NAMES]
        return (by_h[None], *(jnp.stack([mine[number][i] for number in range(layers)]) for i in range(3)))

    states, cut = P(("rep", "r", "s"), None, None), P(None, "s", None)
    return jax.shard_map(
        step,
        mesh=mesh,
        in_specs=(states, states) + (cut,) * 3,
        out_specs=(states,) + (P("rep", "s", None),) * 3,
        check_vma=False,
    )
```

profile of v0, /device:TPU:0, one launch (start us, length us, event | category | flops | bytes accessed | tf_op | source)
XLA Modules:
  0.0 739.4 jit_solution(6884873416927925436)
XLA Ops:
  7.2 0.0 all-gather.13.cloned.1.call-start
  7.2 2.1 fusion.77
  9.3 0.0 all-gather.15.cloned.1.call-start
  9.4 2.1 fusion.78
  11.4 0.0 all-gather.15.cloned.1.call-update
  11.5 0.0 all-gather.17.cloned.1.call-start
  11.5 2.1 fusion.79
  13.6 0.0 all-gather.17.cloned.1.call-update
  13.6 0.0 all-gather.23.cloned.1.call-start
  13.6 0.5 all-gather.23.cloned.1.call-update
  14.2 0.0 all-gather.21.cloned.1.call-start
  14.2 0.5 all-gather.21.cloned.1.call-update
  14.8 0.0 all-gather.19.cloned.1.call-start
  14.8 0.5 all-gather.19.cloned.1.call-update
  15.3 0.0 reduce-scatter.15.cloned.1.call-start
  15.4 8.6 %copy.10 = bf16[1,4096,768]{1,2,0:T(8,128)(2,1)} copy(bf16[1,4096,768]{2,1,0:T(8,128)(2,1)} %param.5) | data formatting | bytes 12582912 | tf_op args[0]
  24.0 4.1 fusion.15
  28.1 0.6 copy-done.2
  28.7 8.6 %copy.9 = bf16[1,4096,768]{1,2,0:T(8,128)(2,1)} copy(bf16[1,4096,768]{2,1,0:T(8,128)(2,1)} %param.6) | data formatting | bytes 12582912 | tf_op args[1]
  37.3 7.8 %all-gather.13.cloned.1.call-done = bf16[1,768,2048]{2,1,0:T(8,128)(2,1)} async-done(((bf16[1,96,2048]{2,1,0:T(8,128)(2,1)}), bf16[1,768,2048]{2,1,0:T(8,128)(2,1)}) %all-gather.13.cloned.1.call-update) | async-done | bytes 3145744 | tf_op jit(solution)/shard_map/all_gather | solution.py:28
  45.1 22.1 %fusion.42 = f32[4096,2048]{1,0:T(8,128)} fusion(bf16[1,4096,768]{1,2,0:T(8,128)(2,1)} %copy.10, f32[4096]{0:T(1024)S(1)} %fusion.70, bf16[1,768,2048]{2,1,0:T(8,128)(2,1)} %all-gather.13.cloned.1.call-done), kind=kOutput, calls=%fused_computation.61 | convolution fusion | flops 12894339072 | bytes 43008000 | tf_op jit(solution)/shard_map/dot_general | solution.py:21
  67.3 11.7 %all-gather.15.cloned.1.call-done = bf16[1,768,2048]{2,1,0:T(8,128)(2,1)} async-done(((bf16[1,96,2048]{2,1,0:T(8,128)(2,1)}), bf16[1,768,2048]{2,1,0:T(8,128)(2,1)}) %all-gather.15.cloned.1.call-update) | async-done | bytes 3145744 | tf_op jit(solution)/shard_map/all_gather | solution.py:28
  79.0 34.3 %multiply_convert_fusion.1 = (bf16[4096,2048]{1,0:T(8,128)(2,1)}, f32[4096,2048]{1,0:T(8,128)}) fusion(f32[4096,2048]{1,0:T(8,128)} %fusion.42, bf16[1,768,2048]{2,1,0:T(8,128)(2,1)} %all-gather.15.cloned.1.call-done, bf16[1,4096,768]{1,2,0:T(8,128)(2,1)} %copy.10, f32[4096]{0:T(1024)S(1)} %fusion.70), kind=kOutput, calls=%fused_computation.13 | convolution fusion | flops 12944670720 | bytes 93339648 | tf_op jit(solution)/shard_map/dot_general | solution.py:22
  113.3 21.4 %fusion.18 = (f32[4096]{0:T(1024)S(1)}, bf16[4096,768]{0,1:T(8,128)(2,1)}) fusion(bf16[4096,2048]{1,0:T(8,128)(2,1)} %get-tuple-element.20, bf16[1,2048,768]{2,1,0:T(8,128)(2,1)} %all-gather.17.cloned.1.call-done, bf16[1,4096,768]{1,2,0:T(8,128)(2,1)} %copy.10), kind=kOutput, calls=%fused_computation.40 | convolution fusion | flops 12900626432 | bytes 32522240 | tf_op jit(solution)/shard_map/dot_general | solution.py:10
  134.7 12.3 %all-gather.23.cloned.1.call-done = bf16[1,768,2048]{2,1,0:T(8,128)(2,1)} async-done(((bf16[1,96,2048]{2,1,0:T(8,128)(2,1)}), bf16[1,768,2048]{2,1,0:T(8,128)(2,1)}) %all-gather.23.cloned.1.call-update) | async-done | bytes 3145744 | tf_op jit(solution)/shard_map/all_gather | solution.py:28
  147.1 22.5 %fusion.33 = f32[4096,2048]{1,0:T(8,128)} fusion(bf16[4096,768]{0,1:T(8,128)(2,1)} %get-tuple-element.23, f32[4096]{0:T(1024)S(1)} %fusion.71, bf16[1,768,2048]{2,1,0:T(8,128)(2,1)} %all-gather.23.cloned.1.call-done), kind=kOutput, calls=%fused_computation.57 | convolution fusion | flops 12894339072 | bytes 43008000 | tf_op jit(solution)/shard_map/jvp()/dot_general | solution.py:22
  169.6 11.1 %all-gather.21.cloned.1.call-done = bf16[1,2048,768]{2,1,0:T(8,128)(2,1)} async-done(((bf16[1,256,768]{2,1,0:T(8,128)(2,1)}), bf16[1,2048,768]{2,1,0:T(8,128)(2,1)}) %all-gather.21.cloned.1.call-update) | async-done | bytes 3145744 | tf_op jit(solution)/shard_map/all_gather | solution.py:28
  180.7 20.1 %convolution_convert_fusion.1 = bf16[4096,2048]{1,0:T(8,128)(2,1)} fusion(bf16[1,4096,768]{2,1,0:T(8,128)(2,1)} %param.6, bf16[1,2048,768]{2,1,0:T(8,128)(2,1)} %all-gather.21.cloned.1.call-done), kind=kOutput, calls=%fused_computation.32 | convolution fusion | flops 12893290496 | bytes 26214400 | tf_op jit(solution)/shard_map/transpose(jvp())/dot_general | solution.py:10
  200.8 14.2 %all-gather.19.cloned.1.call-done = bf16[1,768,2048]{2,1,0:T(8,128)(2,1)} async-done(((bf16[1,96,2048]{2,1,0:T(8,128)(2,1)}), bf16[1,768,2048]{2,1,0:T(8,128)(2,1)}) %all-gather.19.cloned.1.call-update) | async-done | bytes 3145744 | tf_op jit(solution)/shard_map/all_gather | solution.py:28
  215.0 45.2 %fusion.1 = (bf16[4096,2048]{1,0:T(8,128)(2,1)}, f32[4096,2048]{1,0:T(8,128)}) fusion(f32[4096,2048]{1,0:T(8,128)} %fusion.33, bf16[4096,2048]{1,0:T(8,128)(2,1)} %convolution_convert_fusion.1, bf16[1,768,2048]{2,1,0:T(8,128)(2,1)} %all-gather.19.cloned.1.call-done, bf16[4096,768]{0,1:T(8,128)(2,1)} %get-tuple-element.23, f32[4096]{0:T(1024)S(1)} %fusion.71), kind=kOutput, calls=%fused_computation.7 | convolution fusion | flops 12995002368 | bytes 110116864 | tf_op jit(solution)/shard_map/jvp()/dot_general | solution.py:21
  260.2 25.2 %fusion.22 = bf16[4096,768]{0,1:T(8,128)(2,1)} fusion(bf16[4096,2048]{1,0:T(8,128)(2,1)} %convolution_convert_fusion.1, bf16[1,768,2048]{2,1,0:T(8,128)(2,1)} %all-gather.23.cloned.1.call-done, f32[4096,2048]{1,0:T(8,128)} %get-tuple-element.25), kind=kOutput, calls=%fused_computation.44 | convolution fusion | flops 12938379264 | bytes 59768832 | tf_op jit(solution)/shard_map/transpose(jvp())/dot_general | solution.py:22
  285.5 25.2 %fusion.20 = (f32[4096]{0:T(1024)S(1)}, bf16[4096,768]{0,1:T(8,128)(2,1)}) fusion(bf16[4096,768]{0,1:T(8,128)(2,1)} %get-tuple-element.23, bf16[4096,768]{0,1:T(8,128)(2,1)} %fusion.22, bf16[4096,2048]{1,0:T(8,128)(2,1)} %get-tuple-element.24, bf16[1,768,2048]{2,1,0:T(8,128)(2,1)} %all-gather.19.cloned.1.call-done), kind=kOutput, calls=%fused_computation.42 | convolution fusion | flops 12900626432 | bytes 38813696 | tf_op jit(solution)/shard_map/transpose(jvp())/dot_general | solution.py:21
  310.7 6.7 fusion.25
  317.4 2.6 copy-done.1
  320.0 18.4 %convolution_convert_fusion.5 = bf16[2048,768]{1,0:T(8,128)(2,1)} fusion(bf16[4096,2048]{1,0:T(8,128)(2,1)} %get-tuple-element.20, bf16[4096,768]{0,1:T(8,128)(2,1)S(1)} %fusion.25), kind=kOutput, calls=%fused_computation.62 | convolution fusion | flops 12886474752 | bytes 26214400 | tf_op jit(solution)/shard_map/transpose(jvp())/dot_general | solution.py:10
  338.4 0.0 reduce-scatter.15.cloned.1.call-update
  338.4 0.0 reduce-scatter.17.cloned.1.call-start
  338.5 28.0 %fusion.50 = bf16[2048,768]{1,0:T(8,128)(2,1)} fusion(bf16[1,4096,768]{2,1,0:T(8,128)(2,1)} %param.6, f32[4096,2048]{1,0:T(8,128)} %fusion.33, f32[4096,2048]{1,0:T(8,128)} %get-tuple-element.25), kind=kOutput, calls=%fused_computation.65 | convolution fusion | flops 12936806400 | bytes 76546048 | tf_op jit(solution)/shard_map/transpose(jvp())/dot_general | solution.py:10
  366.4 0.0 reduce-scatter.17.cloned.1.call-update
  366.5 0.0 reduce-scatter.11.cloned.1.call-start
  366.5 42.1 %fusion.3 = (bf16[4096,2048]{1,0:T(8,128)(2,1)}, bf16[4096,2048]{1,0:T(8,128)(2,1)}) fusion(f32[4096,2048]{1,0:T(8,128)} %fusion.42, f32[4096,2048]{1,0:T(8,128)} %get-tuple-element.21, bf16[4096,768]{0,1:T(8,128)(2,1)} %copy-done.1, bf16[1,2048,768]{2,1,0:T(8,128)(2,1)} %all-gather.17.cloned.1.call-done), kind=kOutput, calls=%fused_computation.9 | convolution fusion | flops 12993953792 | bytes 110100480 | tf_op jit(solution)/shard_map/transpose(jvp())/dot_general | solution.py:10
  408.6 21.7 %fusion.53 = bf16[768,2048]{1,0:T(8,128)(2,1)} fusion(bf16[4096,2048]{1,0:T(8,128)(2,1)} %get-tuple-element.29, bf16[1,4096,768]{1,2,0:T(8,128)(2,1)S(1)} %bitcast.83, f32[4096]{0:T(1024)S(1)} %copy-done.5, f32[4096,2048]{1,0:T(8,128)} %fusion.42), kind=kOutput, calls=%fused_computation.66 | convolution fusion | flops 12946243584 | bytes 59785216 | tf_op jit(solution)/shard_map/transpose(jvp())/dot_general | solution.py:22
  430.4 0.0 reduce-scatter.11.cloned.1.call-update
  430.4 0.0 reduce-scatter.13.cloned.1.call-start
  430.5 23.6 %fusion.56 = bf16[768,2048]{1,0:T(8,128)(2,1)} fusion(bf16[4096,2048]{1,0:T(8,128)(2,1)} %convolution_convert_fusion.1, bf16[4096,768]{0,1:T(8,128)(2,1)} %get-tuple-element.23, f32[4096]{0:T(1024)S(1)} %copy-done.7, f32[4096,2048]{1,0:T(8,128)} %get-tuple-element.25), kind=kOutput, calls=%fused_computation.67 | convolution fusion | flops 12946243584 | bytes 59785216 | tf_op jit(solution)/shard_map/transpose(jvp())/dot_general | solution.py:22
  454.1 0.0 reduce-scatter.13.cloned.1.call-update
  454.1 0.0 reduce-scatter.9.cloned.1.call-start
  454.1 19.9 %fusion.47 = bf16[768,2048]{1,0:T(8,128)(2,1)} fusion(bf16[4096,2048]{1,0:T(8,128)(2,1)} %get-tuple-element.24, bf16[4096,768]{0,1:T(8,128)(2,1)} %get-tuple-element.23, f32[4096]{0:T(1024)S(1)} %copy-done.7), kind=kOutput, calls=%fused_computation.64 | convolution fusion | flops 12894339072 | bytes 26230784 | tf_op jit(solution)/shard_map/transpose(jvp())/dot_general | solution.py:21
  474.0 0.0 reduce-scatter.9.cloned.1.call-update
  474.1 0.0 reduce-scatter.7.cloned.1.call-start
  474.1 19.7 %fusion.44 = bf16[768,2048]{1,0:T(8,128)(2,1)} fusion(bf16[4096,2048]{1,0:T(8,128)(2,1)} %get-tuple-element.28, bf16[1,4096,768]{1,2,0:T(8,128)(2,1)} %copy.10, f32[4096]{0:T(1024)S(1)} %copy-done.5), kind=kOutput, calls=%fused_computation.63 | convolution fusion | flops 12894339072 | bytes 26230784 | tf_op jit(solution)/shard_map/transpose(jvp())/dot_general | solution.py:21
  493.8 0.0 reduce-scatter.7.cloned.1.call-update
  493.8 0.0 all-reduce.3.cloned.1.call-start
  493.9 25.5 %fusion.21 = bf16[4096,768]{0,1:T(8,128)(2,1)} fusion(bf16[4096,2048]{1,0:T(8,128)(2,1)} %get-tuple-element.29, bf16[1,768,2048]{2,1,0:T(8,128)(2,1)} %all-gather.15.cloned.1.call-done, f32[4096,2048]{1,0:T(8,128)} %fusion.42), kind=kOutput, calls=%fused_computation.43 | convolution fusion | flops 12938379264 | bytes 59768832 | tf_op jit(solution)/shard_map/transpose(jvp())/dot_general | solution.py:22
  519.4 12.6 %reduce-scatter.13.cloned.1.call-done = bf16[96,2048]{1,0:T(8,128)(2,1)} async-done(((bf16[768,2048]{1,0:T(8,128)(2,1)}), bf16[96,2048]{1,0:T(8,128)(2,1)}) %reduce-scatter.13.cloned.1.call-update) | async-done | bytes 393232 | tf_op jit(solution)/shard_map/reduce_scatter | solution.py:31
  532.0 49.3 %reduce-scatter.9.cloned.1.call-done = bf16[96,2048]{1,0:T(8,128)(2,1)} async-done(((bf16[768,2048]{1,0:T(8,128)(2,1)}), bf16[96,2048]{1,0:T(8,128)(2,1)}) %reduce-scatter.9.cloned.1.call-update) | async-done | bytes 393232 | tf_op jit(solution)/shard_map/reduce_scatter | solution.py:31
  581.3 49.1 %reduce-scatter.7.cloned.1.call-done = bf16[96,2048]{1,0:T(8,128)(2,1)} async-done(((bf16[768,2048]{1,0:T(8,128)(2,1)}), bf16[96,2048]{1,0:T(8,128)(2,1)}) %reduce-scatter.7.cloned.1.call-update) | async-done | bytes 393232 | tf_op jit(solution)/shard_map/reduce_scatter | solution.py:31
  630.4 0.0 all-reduce.3.cloned.1.call-update
  630.4 20.9 %fusion.17 = (f32[4096]{0:T(1024)S(1)}, bf16[4096,768]{0,1:T(8,128)(2,1)S(1)}) fusion(bf16[1,4096,768]{1,2,0:T(8,128)(2,1)} %copy.10, bf16[4096,768]{0,1:T(8,128)(2,1)} %fusion.21, bf16[4096,2048]{1,0:T(8,128)(2,1)} %get-tuple-element.28, bf16[1,768,2048]{2,1,0:T(8,128)(2,1)} %all-gather.13.cloned.1.call-done), kind=kOutput, calls=%fused_computation.39 | convolution fusion | flops 12900626432 | bytes 38813696 | tf_op jit(solution)/shard_map/transpose(jvp())/dot_general | solution.py:21
  651.4 9.6 %fusion.24 = bf16[1,4096,768]{1,2,0:T(8,128)(2,1)} fusion(bf16[4096,768]{0,1:T(8,128)(2,1)} %copy-done.1, bf16[4096,768]{0,1:T(8,128)(2,1)S(1)} %get-tuple-element.31, bf16[1,4096,768]{1,2,0:T(8,128)(2,1)} %copy.10, f32[4096]{0:T(1024)S(1)} %multiply_multiply_fusion, f32[4096]{0:T(1024)S(1)} %copy-done.5), kind=kLoop, calls=%fused_computation.49 | loop fusion | flops 22020096 | bytes 25198592 | tf_op jit(solution)/shard_map/broadcast_in_dim | solution.py:44
  661.0 8.6 %copy.11 = bf16[1,4096,768]{2,1,0:T(8,128)(2,1)} copy(bf16[1,4096,768]{1,2,0:T(8,128)(2,1)} %fusion.24) | data formatting | bytes 12582912
  669.6 58.2 %all-reduce.3.cloned.1.call-done = (bf16[1,96,2048]{2,1,0:T(8,128)(2,1)}, bf16[1,96,2048]{2,1,0:T(8,128)(2,1)}, bf16[1,96,2048]{2,1,0:T(8,128)(2,1)}, bf16[1,96,...) async-done(((bf16[1,96,2048]{2,1,0:T(8,128)(2,1)}, bf16[1,96,2048]{2,1,0:T(8,128)(2,1)}, bf16[1,96,2048]{2,1,0:T(8,128)(2,1)}, ...) | async-done | bytes 2359312 | tf_op jit(solution)/shard_map/psum | solution.py:31
  727.7 2.1 pad_maximum_fusion.2
  729.8 2.6 pad_maximum_fusion
  (32 shorter events, 0.1 us)
Async XLA Ops:
  7.2 38.0 %all-gather.13.cloned.1.call-start = ((), (), s32[]{:S(2)}) async-start(), calls=%async_computation.12 | async-start | bytes 3538944 | tf_op jit(solution)/shard_map/all_gather | solution.py:28
  9.3 69.7 %all-gather.15.cloned.1.call-start = ((), (), s32[]{:S(2)}) async-start(), calls=%async_computation.13 | async-start | bytes 3538944 | tf_op jit(solution)/shard_map/all_gather | solution.py:28
  11.5 101.9 %all-gather.17.cloned.1.call-start = ((), (), s32[]{:S(2)}) async-start(), calls=%async_computation.14 | async-start | bytes 3538944 | tf_op jit(solution)/shard_map/all_gather | solution.py:28
  13.6 133.5 %all-gather.23.cloned.1.call-start = ((), (), s32[]{:S(2)}) async-start(), calls=%async_computation.17 | async-start | bytes 3538944 | tf_op jit(solution)/shard_map/all_gather | solution.py:28
  14.2 166.6 %all-gather.21.cloned.1.call-start = ((), (), s32[]{:S(2)}) async-start(), calls=%async_computation.16 | async-start | bytes 3538944 | tf_op jit(solution)/shard_map/all_gather | solution.py:28
  14.8 200.2 %all-gather.19.cloned.1.call-start = ((), (), s32[]{:S(2)}) async-start(), calls=%async_computation.15 | async-start | bytes 3538944 | tf_op jit(solution)/shard_map/all_gather | solution.py:28
  15.3 504.1 %reduce-scatter.15.cloned.1.call-start = ((), (), s32[]{:S(2)}) async-start(), calls=%async_computation.10 | async-start | bytes 3538944 | tf_op jit(solution)/shard_map/reduce_scatter | solution.py:31
  28.1 0.6 copy-start.2
  28.7 50.3 %copy-start.4 = (f32[4096]{0:T(1024)}, f32[4096]{0:T(1024)S(1)}, u32[]{:S(2)}) copy-start(f32[4096]{0:T(1024)S(1)} %fusion.70) | copy-start | bytes 49156
  134.7 34.9 %copy-start.8 = (f32[4096]{0:T(1024)}, f32[4096]{0:T(1024)S(1)}, u32[]{:S(2)}) copy-start(f32[4096]{0:T(1024)S(1)} %get-tuple-element.22) | copy-start | bytes 49156
  134.7 175.9 %copy-start.6 = (f32[4096]{0:T(1024)}, f32[4096]{0:T(1024)S(1)}, u32[]{:S(2)}) copy-start(f32[4096]{0:T(1024)S(1)} %fusion.71) | copy-start | bytes 49156
  285.4 25.2 %copy-start.9 = (f32[4096]{0:T(1024)S(1)}, f32[4096]{0:T(1024)}, u32[]{:S(2)}) copy-start(f32[4096]{0:T(1024)} %copy-done.8) | copy-start | bytes 49156
  285.5 25.2 %copy-start = (bf16[1,4096,768]{1,2,0:T(8,128)(2,1)S(1)}, bf16[1,4096,768]{1,2,0:T(8,128)(2,1)}, u32[]{:S(2)}) copy-start(bf16[1,4096,768]{1,2,0:T(8,128)(2,1)} %copy.9) | copy-start | bytes 18874372
  317.4 2.6 copy-start.1
  338.4 181.0 %reduce-scatter.17.cloned.1.call-start = ((), (), s32[]{:S(2)}) async-start(), calls=%async_computation.11 | async-start | bytes 3538944 | tf_op jit(solution)/shard_map/reduce_scatter | solution.py:31
  338.5 70.1 %slice-start = ((s8[6291456]{0:T(1024)(128)(4,1)}), s8[2097152]{0:T(1024)(128)(4,1)S(1)}, s32[]{:S(2)}) async-start(s8[6291456]{0:T(1024)(128)(4,1)} %bitcast.82), calls=%async_computation.19 | async-start | bytes 4194304
  366.5 152.9 %reduce-scatter.11.cloned.1.call-start = ((), (), s32[]{:S(2)}) async-start(), calls=%async_computation.8 | async-start | bytes 3538944 | tf_op jit(solution)/shard_map/reduce_scatter | solution.py:31
  366.5 42.1 %slice-start.1 = ((s8[6291456]{0:T(1024)(128)(4,1)}), s8[4194304]{0:T(1024)(128)(4,1)S(1)}, s32[]{:S(2)}) async-start(s8[6291456]{0:T(1024)(128)(4,1)} %bitcast.82), calls=%async_computation.20 | async-start | bytes 8388608
  366.5 42.1 %copy-start.5 = (f32[4096]{0:T(1024)S(1)}, f32[4096]{0:T(1024)}, u32[]{:S(2)}) copy-start(f32[4096]{0:T(1024)} %copy-done.4) | copy-start | bytes 49156
  408.6 21.8 %copy-start.7 = (f32[4096]{0:T(1024)S(1)}, f32[4096]{0:T(1024)}, u32[]{:S(2)}) copy-start(f32[4096]{0:T(1024)} %copy-done.6) | copy-start | bytes 49156
  430.4 101.6 %reduce-scatter.13.cloned.1.call-start = ((), (), s32[]{:S(2)}) async-start(), calls=%async_computation.9 | async-start | bytes 3538944 | tf_op jit(solution)/shard_map/reduce_scatter | solution.py:31
  454.1 127.2 %reduce-scatter.9.cloned.1.call-start = ((), (), s32[]{:S(2)}) async-start(), calls=%async_computation.7 | async-start | bytes 3538944 | tf_op jit(solution)/shard_map/reduce_scatter | solution.py:31
  474.1 156.3 %reduce-scatter.7.cloned.1.call-start = ((), (), s32[]{:S(2)}) async-start(), calls=%async_computation.6 | async-start | bytes 3538944 | tf_op jit(solution)/shard_map/reduce_scatter | solution.py:31
  493.8 233.9 %all-reduce.3.cloned.1.call-start = ((), (), s32[]{:S(2)}) async-start(), calls=%async_computation.18 | async-start | bytes 4718592 | tf_op jit(solution)/shard_map/psum | solution.py:31
  630.4 21.0 %copy-start.3 = (f32[4096]{0:T(1024)S(1)}, f32[4096]{0:T(1024)}, u32[]{:S(2)}) copy-start(f32[4096]{0:T(1024)} %copy-done.2) | copy-start | bytes 49156
Sparse Core Ops, SparseCore 0:
  10.4 34.6 all-gather.12
  47.0 31.8 all-gather.14
  80.9 31.8 all-gather.16
  115.1 31.8 all-gather.22
  148.8 31.8 all-gather.20
  183.0 31.8 all-gather.18
  338.6 45.8 reduce-scatter.14
  387.8 45.8 reduce-scatter.16
  437.1 45.8 reduce-scatter.10
  486.2 45.7 reduce-scatter.12
  535.4 45.8 reduce-scatter.8
  584.5 45.8 reduce-scatter.6
  633.2 94.4 all-reduce.2
where the time goes:
time: 747 us; the launch traced here: 739 us
  matrix products  436 us (58%)
  waiting for transfers between devices  228 us (31%)
  local copies, waits for them, and re-layouts  35.3 us (5%)
  other arithmetic  25.1 us (3%)
  between operations  14.5 us (2%)
    dot_general x6, matrix products, layer(): gate = jnp.dot(a, w['w_gate'], preferred_element_type=jnp.float32)  153 us
    dot_general x6, matrix products, layer(): up = jnp.dot(a, w['w_up'], preferred_element_type=jnp.float32)  153 us
    dot_general x5, matrix products, matmul(): jnp.dot(a, w, preferred_element_type=jnp.float32).astype(jnp.bfloat16)  130 us
    reduce_scatter x6, waiting for transfers between devices, summed(): lax.psum_scatter(term, 's', scatter_dimension=0, tiled=True)  111 us
    psum x1, waiting for transfers between devices, summed(): lax.psum(lax.psum_scatter(term, 's', scatter_dimension=0, tiled=True), 'r')  58.2 us
    all_gather x6, waiting for transfers between devices, fetched(): lax.all_gather(w[number], 's', axis=0, tiled=True)  57.2 us
    unnamed x27, local copies, waits for them, and re-layouts  29.1 us
  transfers between devices with their start and end apart: 13, of which 9 were waited for; matrix products, arithmetic and copies ran while one was open for 49% of the time, Pallas kernels for 0%

commit v1 on v0

v1 whole, which is shorter than its diff:
```python
import functools

import jax
import jax.numpy as jnp
from jax import lax
from jax.experimental import pallas as pl
from jax.experimental.pallas import tpu as pltpu
from jax.sharding import PartitionSpec as P

N, D, FF = 4096, 768, 2048
C, NC = 256, 8
WIDE, BOTH = 2 * C, 2 * FF
QUARTER, PIECE, HALF = C // 2, C // 4, C // 8
ROWS = D // NC
UNITS = 24
PER = UNITS // 2
LAST = 17
OTHERS = (1, 2, 3)
T0, T1, T2, T3, T4, T5 = FF, WIDE, FF, WIDE, FF, WIDE
S0, S1, S2, S3, S4, S5 = 4, 2, 4, 2, 4, 2
M3 = 4
f32, bf16 = jnp.float32, jnp.bfloat16
NN = (((1,), (0,)), ((), ()))
NT = (((1,), (1,)), ((), ()))
TN = (((0,), (0,)), ((), ()))
MESH = pl.DeviceIdType.MESH
VMEM, SEM = pltpu.VMEM, pltpu.SemaphoreType.DMA
PAIR = SEM((2,))
local = pltpu.make_async_copy


def dot(a, b, dims=NN):
    return lax.dot_general(a, b, dims, preferred_element_type=f32)


def scale_of(wide):
    return lax.rsqrt(jnp.mean(wide * wide, -1, keepdims=True) + 1e-6)


def normed(h):
    wide = h.astype(f32)
    return (wide * scale_of(wide)).astype(bf16)


def norm_back(h, by_a, by_out):
    wide = h.astype(f32)
    by_a = by_a.astype(bf16).astype(f32)
    scale = scale_of(wide)
    along = jnp.mean(by_a * wide, -1, keepdims=True) * (scale * scale * scale)
    return (by_out.astype(f32) + (by_a * scale - wide * along).astype(bf16).astype(f32)).astype(bf16)


def back(g, u, dp):
    dp = dp.astype(bf16).astype(f32)
    s = jax.nn.sigmoid(g)
    sg = g * s
    return jnp.concatenate([(dp * u * (s + sg * (1 - s))).astype(bf16), (dp * sg).astype(bf16)], 1), sg * u


def times(start, size):
    return pl.ds(pl.multiple_of(start * size, size), size)


def loop(count, body):
    def step(i, carry):
        body(i)
        return carry

    lax.fori_loop(0, count, step, 0)


def fetch(i, count, copies):
    @pl.when(i == 0)
    def _():
        for c in copies(i):
            c.start()

    @pl.when(i + 1 < count)
    def _():
        for c in copies(i + 1):
            c.start()


def arrive(copies):
    for c in copies:
        c.wait()


def again(i, copy):
    pl.when(i >= 2)(copy.wait)


def added(t, ref, term):
    return jnp.where(t == 0, 0.0, ref) + term


def kernel(x, dy, wg, wu, wd, dx, og, od, gus, ps, dgus, h1s, a0s, dws, A, DY, WGU, WD, lsem, go):
    x_in, dy_in = local(x, A, lsem.at[0]), local(dy, DY, lsem.at[1])
    a_out, a_in = local(A, a0s, lsem.at[0]), local(a0s, A, lsem.at[0])
    x_in.start()
    dy_in.start()
    go.open()
    x_in.wait()

    @functools.partial(loop, N // C)
    def _(t):
        A[times(t, C), :] = normed(A[times(t, C), :])

    a_out.start()
    go.weights_first()

    def forward(hid, sp):
        pl.run_scoped(functools.partial(hidden0, hid), VMEM((2, T0, WIDE), f32), PAIR)
        a_out.wait()
        local(hid, ps, sp).start()
        pl.run_scoped(functools.partial(states1, hid), VMEM((2, T1, D), bf16), VMEM((2, T1, D), bf16), PAIR, PAIR)
        local(hid, ps, sp).wait()

    def hidden0(hid, stg, ss):
        B, nt = T0 // S0, N // T0

        def leave(it):
            return local(stg.at[it % 2], gus.at[it // nt, times(it % nt, T0)], ss.at[it % 2])

        def tile(it):
            j, t, slot = it // nt, it % nt, it % 2
            again(it, leave(it))
            go.step0(it)
            w = WGU[0, :, times(j, WIDE)]
            for k in range(S0):
                gu = dot(A[pl.ds(t * T0 + k * B, B), :], w)
                stg[slot, pl.ds(k * B, B)] = gu
                g, u = gu[:, :C], gu[:, C:]
                hid[pl.ds(t * T0 + k * B, B), times(j, C)] = (g * jax.nn.sigmoid(g) * u).astype(bf16)
            leave(it).start()

        loop(NC * nt, tile)
        arrive(map(leave, range(2)))

    def states1(hid, stx, sth, ss, sx):
        B, nt = T1 // S1, N // T1

        def come(t):
            return [local(x.at[times(t, T1)], stx.at[t % 2], sx.at[t % 2])]

        def leave(t):
            return local(sth.at[t % 2], h1s.at[times(t, T1)], ss.at[t % 2])

        def tile(t):
            slot = t % 2
            fetch(t, nt, come)
            again(t, leave(t))
            arrive(come(t))
            go.step1(t)
            for k in range(S1):
                m = dot(hid[pl.ds(t * T1 + k * B, B), :], WD[0]).astype(bf16)
                h = (stx[slot, pl.ds(k * B, B)].astype(f32) + m.astype(f32)).astype(bf16)
                sth[slot, pl.ds(k * B, B)] = h
                A[pl.ds(t * T1 + k * B, B), :] = normed(h)
            leave(t).start()

        loop(nt, tile)
        arrive(map(leave, range(2)))

    pl.run_scoped(forward, VMEM((N, FF), bf16), SEM)

    def backward(ACC, *sums):
        go.sums(ACC, *sums)
        dy_in.wait()

        def last_layer(acc, stg, ss, sd):
            B, nt = T2 // S2, N // T2

            def leave(it):
                return local(stg.at[it % 2], dgus.at[times(it % nt, T2), times(it // nt, WIDE)], ss.at[it % 2])

            def leave_down(j):
                return local(acc.at[j % 2], dws.at[1, j], sd.at[j % 2])

            def tile(it):
                j, t, slot, here = it // nt, it % nt, it % 2, it // nt % 2
                r = times(t, T2)
                again(it, leave(it))
                pl.when((t == 0) & (j >= 2))(leave_down(j).wait)
                go.step2(j, t)
                w, wdn = WGU[1, :, times(j, WIDE)], WD[1, times(j, C), :]
                dgu, p = [], []
                for k in range(S2):
                    rr = pl.ds(t * T2 + k * B, B)
                    gu = dot(A[rr, :], w)
                    by_gu, hidden = back(gu[:, :C], gu[:, C:], dot(DY[rr, :], wdn, NT))
                    stg[slot, pl.ds(k * B, B)] = by_gu
                    dgu.append(by_gu)
                    p.append(hidden.astype(bf16))
                ACC[...] = added(t, ACC[...], dot(A[r, :], jnp.concatenate(dgu), TN))
                acc[here] = added(t, acc[here], dot(jnp.concatenate(p), DY[r, :], TN))
                leave(it).start()

                @pl.when(t == nt - 1)
                def _():
                    leave_down(j).start()
                    go.end2(j)

            loop(NC * nt, tile)
            arrive(map(leave, range(2)))
            arrive(map(leave_down, range(2)))

        pl.run_scoped(last_layer, VMEM((2, C, D), f32), VMEM((2, T2, WIDE), bf16), PAIR, PAIR)

        def first_layer(acc, part, sd, sl):
            go.downs(part, sl)

            def between(sg, sp, sh, *sems):
                B, M, nt = T3 // S3, FF // M3, N // T3

                def come(t):
                    pairs = (dgus, sg), (ps, sp), (h1s, sh)
                    return [local(src.at[times(t, T3)], dst.at[t % 2], sem.at[t % 2]) for (src, dst), sem in zip(pairs, sems)]

                def tile(t):
                    slot = t % 2
                    fetch(t, nt, come)
                    pl.when(t == 0)(a_in.start)
                    arrive(come(t))
                    dh = []
                    for k in range(S3):
                        rr = pl.ds(t * T3 + k * B, B)
                        da = dot(sg[slot, pl.ds(k * B, B), :], WGU[1], NT)
                        dh.append(norm_back(sh[slot, pl.ds(k * B, B)], da, DY[rr, :]))
                        DY[rr, :] = dh[-1]
                    dh = jnp.concatenate(dh)
                    for m in range(M3):
                        c = pl.ds(m * M, M)
                        acc[c, :] = added(t, acc[c, :], dot(sp[slot, :, c], dh, TN))
                    go.step3(t)

                loop(nt, tile)

            pl.run_scoped(between, VMEM((2, T3, BOTH), bf16), VMEM((2, T3, FF), bf16), VMEM((2, T3, D), bf16), PAIR, PAIR, PAIR)
            for s in range(NC):
                local(acc.at[pl.ds(s * C, C)], dws.at[0, s], sd).start()

            def chunks(stg, sin, ss, si):
                B, nt = T4 // S4, N // T4

                def come(it):
                    return [local(gus.at[it // nt, times(it % nt, T4)], sin.at[it % 2], si.at[it % 2])]

                def leave(it):
                    return local(stg.at[it % 2], dgus.at[times(it % nt, T4), times(it // nt, WIDE)], ss.at[it % 2])

                def tile(it):
                    j, t, slot = it // nt, it % nt, it % 2
                    fetch(it, NC * nt, come)
                    again(it, leave(it))
                    go.step4(it)
                    arrive(come(it))
                    wdn = WD[0, times(j, C), :]
                    dgu = []
                    for k in range(S4):
                        dp = dot(DY[pl.ds(t * T4 + k * B, B), :], wdn, NT)
                        gu = sin[slot, pl.ds(k * B, B), :]
                        by_gu, _ = back(gu[:, :C], gu[:, C:], dp)
                        stg[slot, pl.ds(k * B, B)] = by_gu
                        dgu.append(by_gu)
                    ACC[...] = added(t, ACC[...], dot(A[times(t, T4), :], jnp.concatenate(dgu), TN))
                    leave(it).start()

                loop(NC * nt, tile)
                arrive(map(leave, range(2)))

            go.before4(acc, sd)
            a_in.wait()
            pl.run_scoped(chunks, VMEM((2, T4, WIDE), bf16), VMEM((2, T4, WIDE), f32), PAIR, PAIR)

        pl.run_scoped(first_layer, VMEM((FF, D), f32), VMEM((NC, PIECE, D), f32), SEM, SEM)

        def last(sg, sh, so, ss, *sems):
            B, nt = T5 // S5, N // T5

            def come(t):
                pairs = (dgus, sg), (x, sh)
                return [local(src.at[times(t, T5)], dst.at[t % 2], sem.at[t % 2]) for (src, dst), sem in zip(pairs, sems)]

            def leave(t):
                return local(so.at[t % 2], dx.at[times(t, T5)], ss.at[t % 2])

            def tile(t):
                slot = t % 2
                fetch(t, nt, come)
                again(t, leave(t))
                go.step5(t)
                arrive(come(t))
                for k in range(S5):
                    da = dot(sg[slot, pl.ds(k * B, B), :], WGU[0], NT)
                    so[slot, pl.ds(k * B, B)] = norm_back(sh[slot, pl.ds(k * B, B)], da, DY[pl.ds(t * T5 + k * B, B), :])
                leave(t).start()

            loop(nt, tile)
            arrive(map(leave, range(2)))

        pl.run_scoped(last, VMEM((2, T5, BOTH), bf16), VMEM((2, T5, D), bf16), VMEM((2, T5, D), bf16), PAIR, PAIR, PAIR)
        go.close()

    pl.run_scoped(backward, VMEM((D, WIDE), f32), *go.scratch())


class Links:
    def __init__(self, wg, wu, wd, og, od, dws, WGU, WD, CR, XR, ZR, wsem, csem, xsem, zsem, osem, cred):
        self.wg, self.wu, self.wd, self.og, self.od, self.dws, self.WGU, self.WD = wg, wu, wd, og, od, dws, WGU, WD
        self.CR, self.XR, self.ZR = CR, XR, ZR
        self.wsem, self.csem, self.xsem, self.zsem, self.osem, self.cred = wsem, csem, xsem, zsem, osem, cred
        s = lax.axis_index("s")
        self.z, self.s = lax.axis_index("r"), s
        x, y, c = s // 4, (s // 2) % 2, s % 2
        self.c, self.chip = c, s // 2

        def at(x, y, c):
            return 4 * x + 2 * y + c

        self.partner, self.xn, self.yn, self.dn = at(x, y, 1 - c), at(1 - x, y, c), at(x, 1 - y, c), at(1 - x, 1 - y, c)
        self.planes = (self.xn, self.yn, self.dn)

    def to(self, s=None, z=None):
        return (0, self.z if z is None else z, self.s if s is None else s)

    def beyond(self, k):
        return lax.rem(self.z + k, 4)

    def remote(self, src, dst, send, recv, to):
        copy = pltpu.make_async_remote_copy(src, dst, send, recv, device_id=to, device_id_type=MESH)
        copy.start()


    def where(self, u):
        layer, v = u // PER, u % PER
        if layer == 0:
            return layer, v < 8, v if v < 8 else v - 8
        return layer, v == 0 or v >= 5, 0 if v == 0 else (v - 1 if v < 5 else v - 4)

    def piece(self, u, s, half=None):
        layer, gate, k = self.where(u)
        size = ROWS if gate else PIECE
        start, size = (0, size) if half is None else (half * size // 2, size // 2)
        if gate:
            return self.WGU.at[layer, pl.ds(pl.multiple_of(s * ROWS + start, 16), size), pl.ds(k * WIDE, WIDE)]
        return self.WD.at[layer, pl.ds(pl.multiple_of(s * C + k * PIECE + start, 16), size), :]

    def took(self, u, sem, pieces):
        layer, gate, k = self.where(u)
        ref = self.WGU.at[layer, pl.ds(0, ROWS * pieces), pl.ds(0, WIDE)] if gate else self.WD.at[layer, pl.ds(0, PIECE * pieces), :]
        local(ref, ref, sem).wait()

    def own(self, u):
        layer, gate, k = self.where(u)
        sem = self.wsem.at[0, u]
        if gate:
            rows = pl.ds(pl.multiple_of(self.s * ROWS, 16), ROWS)
            local(self.wg.at[layer, :, pl.ds(k * C, C)], self.WGU.at[layer, rows, pl.ds(k * WIDE, C)], sem).start()
            local(self.wu.at[layer, :, pl.ds(k * C, C)], self.WGU.at[layer, rows, pl.ds(k * WIDE + C, C)], sem).start()
        else:
            local(self.wd.at[layer, pl.ds(k * PIECE, PIECE), :], self.piece(u, self.s), sem).start()

    def first(self, u):
        self.took(u, self.wsem.at[0, u], 1)
        mine = self.piece(u, self.s)
        for to, sem in ((self.xn, 2), (self.yn, 2), (self.partner, 4)):
            self.remote(mine, mine, self.wsem.at[1, u], self.wsem.at[sem, u], self.to(to))

    def second(self, u):
        self.took(u, self.wsem.at[2, u], 2)
        for source, half, to in ((self.xn, 0, self.yn), (self.yn, 1, self.xn)):
            ref = self.piece(u, source, half)
            self.remote(ref, ref, self.wsem.at[1, u], self.wsem.at[3, u], self.to(to))
        for source in (self.xn, self.yn):
            ref = self.piece(u, source)
            self.remote(ref, ref, self.wsem.at[1, u], self.wsem.at[4, u], self.to(self.partner))

    def third(self, u):
        self.took(u, self.wsem.at[3, u], 1)
        ref = self.piece(u, self.dn)
        self.remote(ref, ref, self.wsem.at[1, u], self.wsem.at[4, u], self.to(self.partner))

    def whole(self, u):
        self.took(u, self.wsem.at[4, u], 4)

    def pass_on(self, it):
        for u in range(2, LAST):
            if (5 * u - 6) // 3 == it:
                self.second(u)
                self.first(u + 2)
        for u in range(1, LAST):
            if 5 * u // 3 == it:
                self.third(u)

    def open(self):
        self.own(0)
        self.own(1)
        barrier = pltpu.get_barrier_semaphore()
        peers = [self.to(self.partner)] + [self.to(s) for s in self.planes] + [self.to(z=self.beyond(k)) for k in OTHERS]
        for peer in peers:
            pl.semaphore_signal(barrier, inc=1, device_id=peer, device_id_type=MESH)
        pl.semaphore_wait(barrier, len(peers))
        self.first(0)
        self.first(1)
        for u in range(2, UNITS):
            self.own(u)

    def weights_first(self):
        self.second(0)
        self.first(2)
        self.second(1)
        self.first(3)
        self.third(0)

    def step0(self, it):
        for k in range(2 * NC):
            @pl.when(it == k)
            def _():
                self.pass_on(k)
                if k % 2 == 0:
                    self.whole(k // 2)

    def step1(self, t):
        @pl.when(t == 0)
        def _():
            for it in (2 * NC, 2 * NC + 1):
                self.pass_on(it)
            for u in range(NC, PER):
                if 5 * u // 3 >= 2 * NC + 2:
                    self.third(u)
            for u in range(NC, PER):
                self.whole(u)

        for k in range(NC):
            @pl.when(t == k)
            def _():
                for u in range(PER, LAST):
                    if (5 * u - 6) // 3 == k + 2 * NC + 2:
                        self.second(u)
                        self.first(u + 2)
                    if 5 * u // 3 == k + 2 * NC + 2:
                        self.third(u)


    @staticmethod
    def scratch():
        V = VMEM
        return (
            V((2, 4, ROWS, WIDE), bf16),
            V((2, 4, ROWS, WIDE), f32),
            V((4, 3, ROWS, WIDE), bf16),
            V((6, ROWS, WIDE), f32),
            V((4, ROWS, QUARTER), f32),
            V((4, 3, ROWS, QUARTER), bf16),
            V((4, ROWS, QUARTER), f32),
            V((4, ROWS, QUARTER), bf16),
        )

    def sums(self, ACC, CS, OWN, XS, O2, O3, ZS, ZO, F):
        self.ACC, self.CS, self.OWN, self.XS, self.O2, self.O3, self.ZS, self.ZO, self.F = ACC, CS, OWN, XS, O2, O3, ZS, ZO, F

    def done(self, ref, sem):
        local(ref, ref, sem).wait()

    def pack(self, n, block):
        b = n % 2

        @pl.when(n >= 2)
        def _():
            self.done(self.CS.at[b], self.csem.at[0, b])

        for chip in range(4):
            self.CS[b, chip] = block(2 * chip + 1 - self.c).astype(bf16)
            self.OWN[b, chip] = block(2 * chip + self.c)

        @pl.when(n >= 2)
        def _():
            pl.semaphore_wait(self.cred.at[0], 1)

        self.remote(self.CS.at[b], self.CR.at[b], self.csem.at[0, b], self.csem.at[1, b], self.to(self.partner))

    def pack_gate(self, n):
        self.pack(n, lambda s: self.ACC[pl.ds(pl.multiple_of(s * ROWS, 8), ROWS), :])

    def downs(self, part, sem):
        self.part, self.part_sem = part, sem
        self.load_down(1, 0)

    def load_down(self, layer, k):
        local(self.dws.at[layer, :, pl.ds(pl.multiple_of(k * PIECE, 8), PIECE), :], self.part, self.part_sem).start()

    def pack_down(self, n, layer, k):
        self.done(self.part, self.part_sem)

        def block(s):
            rows = []
            for b in range(3):
                cols = slice(b * C, (b + 1) * C)
                rows.append(jnp.concatenate([self.part[s, 0:HALF, cols], self.part[s, HALF:PIECE, cols]], 1))
            return jnp.concatenate(rows, 0)

        self.pack(n, block)

        @pl.when(k < 3)
        def _():
            self.load_down(layer, k + 1)

    def plane(self, n):
        b, xs, xb = n % 2, n % 4, n % 6

        @pl.when(n >= 4)
        def _():
            self.done(self.XS.at[xs], self.xsem.at[0, xs])

        self.done(self.CR.at[b], self.csem.at[1, b])

        def total(chip):
            return self.OWN[b, chip] + self.CR[b, chip].astype(f32)

        for m, s in enumerate(self.planes):
            self.XS[xs, m] = total(s // 2).astype(bf16)
        self.O2[xb] = total(self.chip)

        @pl.when(n + 2 < UNITS)
        def _():
            pl.semaphore_signal(self.cred.at[0], inc=1, device_id=self.to(self.partner), device_id_type=MESH)

        @pl.when(n >= 6)
        def _():
            for m in range(3):
                pl.semaphore_wait(self.cred.at[1 + m], 1)

        for m, s in enumerate(self.planes):
            self.remote(self.XS.at[xs, m], self.XR.at[xb, m], self.xsem.at[0, xs], self.xsem.at[1, xb], self.to(s))

    def line(self, n):
        xb, zb = n % 6, n % 4

        @pl.when(n >= 4)
        def _():
            self.done(self.ZS.at[zb], self.zsem.at[0, zb])

        self.done(self.XR.at[xb], self.xsem.at[1, xb])
        total = self.O2[xb] + self.XR[xb, 0].astype(f32) + self.XR[xb, 1].astype(f32) + self.XR[xb, 2].astype(f32)
        for q in range(4):
            self.O3[q] = total[:, q * QUARTER : (q + 1) * QUARTER]
        self.ZO[zb] = self.O3[self.z]
        for k in OTHERS:
            self.ZS[zb, k - 1] = self.O3[self.beyond(k)].astype(bf16)

        @pl.when(n + 6 < UNITS)
        def _():
            for m, s in enumerate(self.planes):
                pl.semaphore_signal(self.cred.at[1 + m], inc=1, device_id=self.to(s), device_id_type=MESH)

        @pl.when(n >= 4)
        def _():
            for k in OTHERS:
                pl.semaphore_wait(self.cred.at[3 + k], 1)

        for k in OTHERS:
            self.remote(self.ZS.at[zb, k - 1], self.ZR.at[zb, 3 - k], self.zsem.at[0, zb], self.zsem.at[1, zb], self.to(z=self.beyond(k)))

    def final(self, n):
        zb = n % 4

        @pl.when(n >= 4)
        def _():
            self.sent_final(zb)

        self.done(self.ZR.at[zb], self.zsem.at[1, zb])
        total = self.ZO[zb] + self.ZR[zb, 0].astype(f32) + self.ZR[zb, 1].astype(f32) + self.ZR[zb, 2].astype(f32)
        self.F[zb] = total.astype(bf16)

        @pl.when(n + 4 < UNITS)
        def _():
            for k in OTHERS:
                pl.semaphore_signal(self.cred.at[3 + 4 - k], inc=1, device_id=self.to(z=self.beyond(k)), device_id_type=MESH)

        own, other = self.osem.at[1, zb], self.osem.at[0, zb]
        half = self.z // 2
        layer = 1 - n // PER

        def gate(j):
            place = self.og.at[half, layer, :, pl.ds(pl.multiple_of(j * C + self.z % 2 * QUARTER, QUARTER), QUARTER)]
            local(self.F.at[zb], place, own).start()
            for k in OTHERS:
                self.remote(self.F.at[zb], place, other, self.osem.at[2, 0], self.to(z=self.beyond(k)))

        def down(k):
            for b in range(3):
                src = self.F.at[zb, pl.ds(b * HALF, HALF)]
                place = self.od.at[layer, pl.ds(pl.multiple_of(k * PIECE + half * HALF, HALF), HALF), pl.ds(pl.multiple_of(b * C + self.z % 2 * QUARTER, QUARTER), QUARTER)]
                local(src, place, own).start()
                for k_ in OTHERS:
                    self.remote(src, place, other, self.osem.at[2, 1], self.to(z=self.beyond(k_)))

        early = (n >= PER) & (n < 20)
        pl.when((n < 8) | (n >= 20))(lambda: gate(n - 16 * (n // PER)))
        pl.when(early & (n % 2 == 1))(lambda: gate((n - 13) // 2))
        pl.when((n >= 8) & (n < PER))(lambda: down(n - 8))
        pl.when(early & (n % 2 == 0))(lambda: down((n - PER) // 2))

    def sent_final(self, zb):
        self.done(self.F.at[zb], self.osem.at[1, zb])
        ref = self.ZR.at[zb]
        local(ref, ref, self.osem.at[0, zb]).wait()

    def step2(self, j, t):
        for k in range(NC):
            @pl.when((t == 0) & (j == k))
            def _():
                if k == 0:
                    self.third(LAST - 1)
                for u in range(PER if k == 0 else LAST - 1 + k, LAST + k):
                    self.whole(u)
                if LAST + k < UNITS:
                    self.second(LAST + k)
                if LAST + 2 + k < UNITS:
                    self.first(LAST + 2 + k)

            if LAST + k < UNITS:
                @pl.when((t == 1) & (j == k))
                def _():
                    self.third(LAST + k)

        for back, stage in ((3, self.final), (2, self.line), (1, self.plane)):
            @pl.when((t == 1) & (j >= back))
            def _():
                stage(j - back)

    def end2(self, j):
        self.pack_gate(j)

    def step3(self, t):
        for back, stage, last in ((3, self.final, 6), (2, self.line, 5), (1, self.plane, 4)):
            @pl.when(t <= last)
            def _():
                stage(8 + t - back)

        @pl.when(t <= 3)
        def _():
            self.pack_down(8 + t, 1, t)

    def before4(self, acc_d, sem):
        self.acc_d, self.acc_sem = acc_d, sem

    def step4(self, it):
        @pl.when(it == 0)
        def _():
            self.done(self.acc_d, self.acc_sem)
            self.load_down(0, 0)

        for start, stage in ((7, self.final), (5, self.line)):
            @pl.when((it >= start) & ((it - start) % 3 != 1))
            def _():
                stage(PER + (2 * (it - start) + 1) // 3)

        @pl.when((it >= 2) & (it <= 9))
        def _():
            self.plane(PER + it - 2)

        @pl.when((it >= 11) & (it % 2 == 1))
        def _():
            self.plane(20 + (it - 11) // 2)

        @pl.when((it <= 7) & (it % 2 == 1))
        def _():
            self.pack_down(PER + it - 1, 0, (it - 1) // 2)

        @pl.when((it >= 2) & (it <= 8) & (it % 2 == 0))
        def _():
            self.pack_gate(PER + it - 1)

        @pl.when((it >= 10) & (it % 2 == 0))
        def _():
            self.pack_gate(PER + it // 2 + 3)

    def step5(self, t):
        @pl.when((t >= 1) & (t <= 6))
        def _():
            self.final(17 + t)

        @pl.when(t <= 4)
        def _():
            self.line(19 + t)

        @pl.when(t == 1)
        def _():
            self.plane(23)

        @pl.when(t == 0)
        def _():
            self.pack_gate(23)

    def close(self):
        for b in range(2):
            self.done(self.CS.at[b], self.csem.at[0, b])
        for b in range(4):
            self.done(self.XS.at[b], self.xsem.at[0, b])
            self.done(self.ZS.at[b], self.zsem.at[0, b])
            self.sent_final(b)
        for u in range(UNITS):
            self.took(u, self.wsem.at[1, u], 7)
        self.done(self.og.at[:, :, :, pl.ds(0, 3 * FF // 4)], self.osem.at[2, 0])
        self.done(self.od.at[:, pl.ds(0, 3 * C // 4)], self.osem.at[2, 1])


def whole(x, dy, wg, wu, wd, dx, og, od, gus, ps, dgus, h1s, a0s, dws, A, DY, WGU, WD, CR, XR, ZR, lsem, wsem, csem, xsem, zsem, osem, cred):
    links = Links(wg, wu, wd, og, od, dws, WGU, WD, CR, XR, ZR, wsem, csem, xsem, zsem, osem, cred)
    kernel(x, dy, wg, wu, wd, dx, og, od, gus, ps, dgus, h1s, a0s, dws, A, DY, WGU, WD, lsem, links)


def solution(mesh):
    def call(x, dy, wg, wu, wd):
        anywhere = pl.BlockSpec(memory_space=pl.ANY)
        S, V, M = jax.ShapeDtypeStruct, VMEM, SEM
        flops = 17 * 2 * N * D * FF
        out = pl.pallas_call(
            whole,
            in_specs=[anywhere] * 5,
            out_specs=[anywhere] * 9,
            out_shape=[
                S((N, D), bf16),
                S((2, 2, ROWS, FF), bf16),
                S((2, C, D), bf16),
                S((NC, N, WIDE), f32),
                S((N, FF), bf16),
                S((N, BOTH), bf16),
                S((N, D), bf16),
                S((N, D), bf16),
                S((2, 8, C, D), f32),
            ],
            scratch_shapes=[
                V((N, D), bf16),
                V((N, D), bf16),
                V((2, D, BOTH), bf16),
                V((2, FF, D), bf16),
                V((2, 4, ROWS, WIDE), bf16),
                V((6, 3, ROWS, WIDE), bf16),
                V((4, 3, ROWS, QUARTER), bf16),
                M((2,)),
                M((5, UNITS)),
                M((2, 2)),
                M((2, 6)),
                M((2, 4)),
                M((3, 4)),
                pltpu.SemaphoreType.REGULAR((7,)),
            ],
            compiler_params=pltpu.CompilerParams(vmem_limit_bytes=67_000_000, collective_id=0, has_side_effects=True),
            cost_estimate=pl.CostEstimate(flops=flops, bytes_accessed=400_000_000, transcendentals=0),
            name="stack",
        )(x, dy, wg, wu, wd)
        return out[:3]

    def step(x, dy, wg, wu, wd):
        dx, gates, downs = call(x[0], dy[0], wg, wu, wd)
        return dx[None], gates[0], gates[1], downs

    states, cut = P(("rep", "r", "s"), None, None), P(None, "s", None)
    return jax.shard_map(
        step,
        mesh=mesh,
        in_specs=(states, states) + (cut,) * 3,
        out_specs=(states,) + (P("rep", "s", None),) * 3,
        check_vma=False,
    )
```

time: 747 us -> 332 us (0.44); the launches traced: 739 us -> 332 us
  matrix products: 436 us -> 0 us
  Pallas kernels: 0 us -> 322 us
  waiting for transfers between devices: 228 us -> 0 us
  local copies, waits for them, and re-layouts: 35.3 us -> 9.54 us
  other arithmetic: 25.1 us -> 0 us
  between operations: 14.5 us -> 0.64 us
    dot_general x17 -> x0, matrix products: 436 us -> none  [the longest x6 153 us: layer(): gate = jnp.dot(a, w['w_gate'], preferred_element_type=jnp.float32)]
    pallas_call x0 -> x1, Pallas kernels: none -> 322 us  [call(): pl.pallas_call(whole, in_specs=[anywhere] * 5, out_specs=[anywhere] * 9,...]
    reduce_scatter x6 -> x0, waiting for transfers between devices: 111 us -> none  [summed(): lax.psum_scatter(term, 's', scatter_dimension=0, tiled=True)]
    psum x1 -> x0, waiting for transfers between devices: 58.2 us -> none  [summed(): lax.psum(lax.psum_scatter(term, 's', scatter_dimension=0, tiled=True), 'r')]
    all_gather x6 -> x0, waiting for transfers between devices: 57.2 us -> none  [fetched(): lax.all_gather(w[number], 's', axis=0, tiled=True)]
    unnamed x27 -> x4, local copies, waits for them, and re-layouts: 29.1 us -> 6.85 us
    broadcast_in_dim x1 -> x0, other arithmetic: 9.56 us -> none  [step(): by_h[None]]
  transfers between devices with their start and end apart: 13 -> 0, of which waited for: 9 -> 0; matrix products, arithmetic and copies ran while one was open for 49% -> 0% of each run, Pallas kernels for 0% -> 0%
where the time goes in v1:
time: 332 us
  Pallas kernels  322 us (97%)
  local copies, waits for them, and re-layouts  9.54 us (3%)
    pallas_call x1, Pallas kernels, call(): pl.pallas_call(whole, in_specs=[anywhere] * 5, out_specs=[anywhere] * 9,...  322 us
    unnamed x4, local copies, waits for them, and re-layouts  6.85 us

profile of v1, /device:TPU:0, one launch (start us, length us, event | category | flops | bytes accessed | tf_op | source)
XLA Modules:
  0.0 332.1 jit_solution(2032812412404489932)
XLA Ops:
  0.6 322.0 %stack.1 = (bf16[4096,768]{1,0:T(8,128)(2,1)}, bf16[2,2,96,2048]{3,2,1,0:T(8,128)(2,1)}, bf16[2,256,768]{2,1,0:T(8,128)(2,1)}, f32[8,4096,512]{2,1,0:T(8,128)}, ...) custom-call(bf16[4096,768]{1,0:T(8,128)(2,1)} %bitcast.8, ...), custom_call_target="tpu_custom_call" | custom-call | flops 219043332096 | bytes 400000000 | tf_op jit(solution)/shard_map/stack/pallas_call | solution.py:720
  322.6 2.7 slice_bitcast_fusion
  325.3 0.0 copy-start
  325.3 6.0 %copy.11 = bf16[1,4096,768]{2,1,0:T(8,128)(2,1)} copy(bf16[1,4096,768]{2,1,0:T(8,128)(2,1)} %bitcast.7) | data formatting | bytes 12582912
  331.3 0.0 copy-done
  331.3 0.9 copy.12
Async XLA Ops:
  325.3 6.0 %copy-start = (bf16[2,256,768]{2,1,0:T(8,128)(2,1)S(1)}, bf16[2,256,768]{2,1,0:T(8,128)(2,1)}, u32[]{:S(2)}) copy-start(bf16[2,256,768]{2,1,0:T(8,128)(2,1)} %get-tuple-element.19) | copy-start | bytes 2359300

commit v2 on v1

v2 whole, which is shorter than its diff:
```python
import functools

import jax
import jax.numpy as jnp
from jax import lax
from jax.experimental import pallas as pl
from jax.experimental.pallas import tpu as pltpu
from jax.sharding import PartitionSpec as P

N, D, FF = 4096, 768, 2048
C, NC = 256, 8
WIDE, BOTH = 2 * C, 2 * FF
QUARTER, PIECE, HALF = C // 2, C // 4, C // 8
ROWS = D // NC
UNITS = 24
PER = UNITS // 2
DOWNS = (NC, PER + 1)
LAST = 17
OTHERS = (1, 2, 3)
T0, T1, T2, T3, T4, T5 = FF, WIDE, FF, WIDE, FF, WIDE
S0, S1, S2, S3, S4, S5 = 4, 2, 4, 2, 4, 2
M3 = 4
f32, bf16 = jnp.float32, jnp.bfloat16
NN = (((1,), (0,)), ((), ()))
NT = (((1,), (1,)), ((), ()))
TN = (((0,), (0,)), ((), ()))
MESH = pl.DeviceIdType.MESH
VMEM, SEM = pltpu.VMEM, pltpu.SemaphoreType.DMA
PAIR = SEM((2,))
local = pltpu.make_async_copy


def dot(a, b, dims=NN):
    return lax.dot_general(a, b, dims, preferred_element_type=f32)


def scale_of(wide):
    return lax.rsqrt(jnp.mean(wide * wide, -1, keepdims=True) + 1e-6)


def normed(h):
    wide = h.astype(f32)
    return (wide * scale_of(wide)).astype(bf16)


def norm_back(h, by_a, by_out):
    wide = h.astype(f32)
    by_a = by_a.astype(bf16).astype(f32)
    scale = scale_of(wide)
    along = jnp.mean(by_a * wide, -1, keepdims=True) * (scale * scale * scale)
    return (by_out.astype(f32) + (by_a * scale - wide * along).astype(bf16).astype(f32)).astype(bf16)


def back(g, u, dp):
    dp = dp.astype(bf16).astype(f32)
    s = jax.nn.sigmoid(g)
    sg = g * s
    return jnp.concatenate([(dp * u * (s + sg * (1 - s))).astype(bf16), (dp * sg).astype(bf16)], 1), sg * u


def times(start, size):
    return pl.ds(pl.multiple_of(start * size, size), size)


def loop(count, body):
    def step(i, carry):
        body(i)
        return carry

    lax.fori_loop(0, count, step, 0)


def fetch(i, count, copies, started=False):
    @pl.when((i == 0) & (not started))
    def _():
        for c in copies(i):
            c.start()

    @pl.when(i + 1 < count)
    def _():
        for c in copies(i + 1):
            c.start()


def arrive(copies):
    for c in copies:
        c.wait()


def again(i, copy):
    pl.when(i >= 2)(copy.wait)


def gates(ref, layer, cols=slice(None)):
    w = ref[layer, :, :, :, cols]
    return w.reshape(D, w.shape[-1])


def choose(i, cases, low=0):
    if len(cases) == 1:
        return cases[0]()
    half = len(cases) // 2
    pl.when(i < low + half)(lambda: choose(i, cases[:half], low))
    pl.when(i >= low + half)(lambda: choose(i, cases[half:], low + half))


def added(t, ref, term):
    return jnp.where(t == 0, 0.0, ref) + term


def kernel(x, dy, wg, wu, wd, dx, og, od, gus, ps, dgus, h1s, a0s, dws, A, DY, WGU, WD, lsem, go):
    x_in, dy_in = local(x, A, lsem.at[0]), local(dy, DY, lsem.at[1])
    a_out, a_in = local(A, a0s, lsem.at[0]), local(a0s, A, lsem.at[0])
    x_in.start()
    dy_in.start()
    go.open()
    x_in.wait()

    @functools.partial(loop, N // C)
    def _(t):
        A[times(t, C), :] = normed(A[times(t, C), :])

    a_out.start()
    go.weights_first()

    def forward(hid, stg, stx, sth, sp, ss, sx, sh):
        x_tile = states_in(stx, sx)
        arrive_later = x_tile(0)
        for c in arrive_later:
            c.start()
        kept = hidden0(hid, stg, ss)
        a_out.wait()
        local(hid, ps, sp).start()
        states1(hid, stx, sth, x_tile, sh)
        arrive(kept)
        local(hid, ps, sp).wait()

    def states_in(stx, sx):
        return lambda t: [local(x.at[times(t, T1)], stx.at[t % 2], sx.at[t % 2])]

    def hidden0(hid, stg, ss):
        B, nt = T0 // S0, N // T0

        def leave(it):
            return local(stg.at[it % 2], gus.at[it // nt, times(it % nt, T0)], ss.at[it % 2])

        def tile(it):
            j, t, slot = it // nt, it % nt, it % 2
            again(it, leave(it))
            go.step0(it)
            w = gates(WGU, 0, times(j, WIDE))
            for k in range(S0):
                gu = dot(A[pl.ds(t * T0 + k * B, B), :], w)
                stg[slot, pl.ds(k * B, B)] = gu
                g, u = gu[:, :C], gu[:, C:]
                hid[pl.ds(t * T0 + k * B, B), times(j, C)] = (g * jax.nn.sigmoid(g) * u).astype(bf16)
            leave(it).start()

        loop(NC * nt, tile)
        return map(leave, range(2))

    def states1(hid, stx, sth, come, ss):
        B, nt = T1 // S1, N // T1

        def leave(t):
            return local(sth.at[t % 2], h1s.at[times(t, T1)], ss.at[t % 2])

        def tile(t):
            slot = t % 2
            fetch(t, nt, come, True)
            again(t, leave(t))
            arrive(come(t))
            go.step1(t)
            for k in range(S1):
                m = dot(hid[pl.ds(t * T1 + k * B, B), :], WD[0].reshape(FF, D)).astype(bf16)
                h = (stx[slot, pl.ds(k * B, B)].astype(f32) + m.astype(f32)).astype(bf16)
                sth[slot, pl.ds(k * B, B)] = h
                A[pl.ds(t * T1 + k * B, B), :] = normed(h)
            leave(t).start()

        loop(nt, tile)
        arrive(map(leave, range(2)))

    tiles1 = VMEM((2, T1, D), bf16)
    pl.run_scoped(forward, VMEM((N, FF), bf16), VMEM((2, T0, WIDE), f32), tiles1, tiles1, SEM, PAIR, PAIR, PAIR)

    def backward(ACC, *sums):
        go.sums(ACC, *sums)
        dy_in.wait()

        def last_layer(acc, stg, ss, sd):
            B, nt = T2 // S2, N // T2

            def leave(it):
                return local(stg.at[it % 2], dgus.at[times(it % nt, T2), times(it // nt, WIDE)], ss.at[it % 2])

            def leave_down(j):
                return local(acc.at[j % 2], dws.at[j], sd.at[j % 2])

            def tile(it):
                j, t, slot, here = it // nt, it % nt, it % 2, it // nt % 2
                r = times(t, T2)
                again(it, leave(it))
                pl.when((t == 0) & (j >= 2))(leave_down(j).wait)
                go.step2(j, t)
                w, wdn = gates(WGU, 1, times(j, WIDE)), WD[1, j // 2, j % 2]
                dgu, p = [], []
                for k in range(S2):
                    rr = pl.ds(t * T2 + k * B, B)
                    gu = dot(A[rr, :], w)
                    by_gu, hidden = back(gu[:, :C], gu[:, C:], dot(DY[rr, :], wdn, NT))
                    stg[slot, pl.ds(k * B, B)] = by_gu
                    dgu.append(by_gu)
                    p.append(hidden.astype(bf16))
                ACC[...] = added(t, ACC[...], dot(A[r, :], jnp.concatenate(dgu), TN).reshape(ACC.shape))
                acc[here] = added(t, acc[here], dot(jnp.concatenate(p), DY[r, :], TN))
                leave(it).start()

                @pl.when(t == nt - 1)
                def _():
                    leave_down(j).start()
                    go.end2(j)

            loop(NC * nt, tile)
            arrive(map(leave, range(2)))
            arrive(map(leave_down, range(2)))

        pl.run_scoped(last_layer, VMEM((2, C, D), f32), VMEM((2, T2, WIDE), bf16), PAIR, PAIR)

        def first_layer(acc, sl):
            go.downs(acc, sl)

            def between(sg, sp, sh, *sems):
                B, M, nt = T3 // S3, FF // M3, N // T3

                def come(t):
                    pairs = (dgus, sg), (ps, sp), (h1s, sh)
                    return [local(src.at[times(t, T3)], dst.at[t % 2], sem.at[t % 2]) for (src, dst), sem in zip(pairs, sems)]

                def tile(t):
                    slot = t % 2
                    fetch(t, nt, come)
                    pl.when(t == 0)(a_in.start)
                    arrive(come(t))
                    dh = []
                    for k in range(S3):
                        rr = pl.ds(t * T3 + k * B, B)
                        da = dot(sg[slot, pl.ds(k * B, B), :], gates(WGU, 1), NT)
                        dh.append(norm_back(sh[slot, pl.ds(k * B, B)], da, DY[rr, :]))
                        DY[rr, :] = dh[-1]
                    dh = jnp.concatenate(dh)
                    for m in range(M3):
                        c = pl.ds(m * M, M)
                        acc[c, :] = added(t, acc[c, :], dot(sp[slot, :, c], dh, TN))
                    go.step3(t)

                loop(nt, tile)

            pl.run_scoped(between, VMEM((2, T3, BOTH), bf16), VMEM((2, T3, FF), bf16), VMEM((2, T3, D), bf16), PAIR, PAIR, PAIR)

            def chunks(stg, sin, ss, si):
                B, nt = T4 // S4, N // T4

                def come(it):
                    return [local(gus.at[it // nt, times(it % nt, T4)], sin.at[it % 2], si.at[it % 2])]

                def leave(it):
                    return local(stg.at[it % 2], dgus.at[times(it % nt, T4), times(it // nt, WIDE)], ss.at[it % 2])

                def tile(it):
                    j, t, slot = it // nt, it % nt, it % 2
                    fetch(it, NC * nt, come)
                    again(it, leave(it))
                    go.step4(it)
                    arrive(come(it))
                    wdn = WD[0, j // 2, j % 2]
                    dgu = []
                    for k in range(S4):
                        dp = dot(DY[pl.ds(t * T4 + k * B, B), :], wdn, NT)
                        gu = sin[slot, pl.ds(k * B, B), :]
                        by_gu, _ = back(gu[:, :C], gu[:, C:], dp)
                        stg[slot, pl.ds(k * B, B)] = by_gu
                        dgu.append(by_gu)
                    ACC[...] = added(t, ACC[...], dot(A[times(t, T4), :], jnp.concatenate(dgu), TN).reshape(ACC.shape))
                    leave(it).start()

                loop(NC * nt, tile)
                arrive(map(leave, range(2)))

            a_in.wait()
            pl.run_scoped(chunks, VMEM((2, T4, WIDE), bf16), VMEM((2, T4, WIDE), f32), PAIR, PAIR)

        pl.run_scoped(first_layer, VMEM((FF, D), f32), SEM)

        def last(sg, sh, so, ss, *sems):
            B, nt = T5 // S5, N // T5

            def come(t):
                pairs = (dgus, sg), (x, sh)
                return [local(src.at[times(t, T5)], dst.at[t % 2], sem.at[t % 2]) for (src, dst), sem in zip(pairs, sems)]

            def leave(t):
                return local(so.at[t % 2], dx.at[times(t, T5)], ss.at[t % 2])

            def tile(t):
                slot = t % 2
                fetch(t, nt, come)
                again(t, leave(t))
                go.step5(t)
                arrive(come(t))
                for k in range(S5):
                    da = dot(sg[slot, pl.ds(k * B, B), :], gates(WGU, 0), NT)
                    so[slot, pl.ds(k * B, B)] = norm_back(sh[slot, pl.ds(k * B, B)], da, DY[pl.ds(t * T5 + k * B, B), :])
                leave(t).start()

            loop(nt, tile)
            arrive(map(leave, range(2)))

        pl.run_scoped(last, VMEM((2, T5, BOTH), bf16), VMEM((2, T5, D), bf16), VMEM((2, T5, D), bf16), PAIR, PAIR, PAIR)
        go.close()

    pl.run_scoped(backward, VMEM((NC, ROWS, WIDE), f32), *go.scratch())


class Links:
    def __init__(self, wg, wu, wd, og, od, dws, WGU, WD, CR, XR, ZR, wsem, csem, xsem, zsem, osem, cred):
        self.wg, self.wu, self.wd, self.og, self.od, self.dws, self.WGU, self.WD = wg, wu, wd, og, od, dws, WGU, WD
        self.CR, self.XR, self.ZR = CR, XR, ZR
        self.wsem, self.csem, self.xsem, self.zsem, self.osem, self.cred = wsem, csem, xsem, zsem, osem, cred
        s, z = lax.axis_index("s"), lax.axis_index("r")
        self.z, self.s = z, s
        x, y, c = s // 4, s // 2 % 2, s % 2
        self.core, self.chip = c, s // 2
        self.chips = 2 * (1 - x) + y, 2 * x + 1 - y, 2 * (1 - x) + 1 - y
        self.planes = [2 * q + c for q in self.chips]
        self.partner = s + 1 - 2 * c
        self.lines = z + 1 - 2 * (z % 2), (z + 2) % 4

    def to(self, s=None, z=None):
        return (0, self.z if z is None else z, self.s if s is None else s)

    def remote(self, src, dst, send, recv, to):
        pltpu.make_async_remote_copy(src, dst, send, recv, device_id=to, device_id_type=MESH).start()

    def done(self, ref, sem):
        local(ref, ref, sem).wait()


    def kind(self, u):
        if not isinstance(u, int):
            return 1, True, u - LAST + 1
        layer, v = u // PER, u % PER
        if layer == 0:
            return layer, v < NC, v % NC
        return layer, v == 0 or v > 4, v - 4 if v > 4 else max(v - 1, 0)

    def unit(self, u, chip, core, rows=None):
        layer, gate, k = self.kind(u)
        if gate:
            return self.WGU.at[layer, chip, core, rows or slice(None), times(k, WIDE)]
        start, size = (rows.start, rows.size) if rows else (0, PIECE)
        return self.WD.at[layer, chip, core, pl.ds(k * PIECE + start, size), :]

    def own(self, u):
        layer, gate, k = self.kind(u)
        sem = self.wsem.at[0, u]
        if gate:
            for w, side in ((self.wg, 0), (self.wu, C)):
                local(w.at[layer, :, pl.ds(k * C, C)], self.WGU.at[layer, self.chip, self.core, :, pl.ds(k * WIDE + side, C)], sem).start()
        elif k == 0:
            local(self.wd.at[layer], self.WD.at[layer, self.chip, self.core], sem).start()

    def first(self, u):
        layer, gate, k = self.kind(u)
        mine = self.unit(u, self.chip, self.core)
        if gate:
            self.done(mine, self.wsem.at[0, u])
        elif k == 0:
            self.done(self.WD.at[layer, self.chip, self.core], self.wsem.at[0, u])
        for to in self.planes[:2]:
            self.remote(mine, mine, self.wsem.at[1, u], self.wsem.at[2, u], self.to(to))

    def second(self, u):
        self.done(self.unit(u, 0, pl.ds(0, 2)), self.wsem.at[2, u])
        size = (ROWS if self.kind(u)[1] else PIECE) // 2
        for half in range(2):
            ref = self.unit(u, self.chips[half], self.core, pl.ds(half * size, size))
            self.remote(ref, ref, self.wsem.at[1, u], self.wsem.at[3, u], self.to(self.planes[1 - half]))

    def third(self, u):
        self.done(self.unit(u, 0, 0), self.wsem.at[3, u])
        ref = self.unit(u, slice(None), self.core)
        self.remote(ref, ref, self.wsem.at[5, u], self.wsem.at[4, u], self.to(self.partner))

    def whole(self, u):
        self.done(self.unit(u, slice(None), 0), self.wsem.at[4, u])

    def pass_on(self, it):
        for u in range(2, LAST):
            if (5 * u - 6) // 3 == it:
                self.second(u)
                self.first(u + 2)
        for u in range(1, LAST):
            if 5 * u // 3 == it:
                self.third(u)

    def open(self):
        self.own(0)
        self.own(1)
        barrier = pltpu.get_barrier_semaphore()
        peers = [self.to(self.partner)] + [self.to(s) for s in self.planes] + [self.to(z=z) for z in self.lines]
        for peer in peers:
            pl.semaphore_signal(barrier, inc=1, device_id=peer, device_id_type=MESH)
        pl.semaphore_wait(barrier, len(peers))
        self.first(0)
        self.first(1)
        for u in range(2, NC + 1):
            self.own(u)

    def weights_first(self):
        self.second(0)
        self.first(2)
        self.second(1)
        self.first(3)
        self.third(0)

    def step0(self, it):
        def case(k):
            self.pass_on(k)
            if k % 2 == 0:
                self.whole(k // 2)
            if PER + k < UNITS:
                self.own(PER + k)

        choose(it, [functools.partial(case, k) for k in range(2 * NC)])

    def step1(self, t):
        def case(k):
            if k == 0:
                self.pass_on(2 * NC)
                self.pass_on(2 * NC + 1)
                for u in range(NC, PER):
                    if 5 * u // 3 >= 2 * NC + 2:
                        self.third(u)
                for u in range(NC, PER):
                    self.whole(u)
            for u in range(PER, LAST):
                if (5 * u - 6) // 3 == k + 2 * NC + 2:
                    self.second(u)
                    self.first(u + 2)
                if 5 * u // 3 == k + 2 * NC + 2:
                    self.third(u)

        choose(t, [functools.partial(case, k) for k in range(NC)])


    @staticmethod
    def scratch():
        blocks, wide = (4, ROWS, WIDE), (ROWS, WIDE)
        return (
            VMEM((2, *blocks), bf16),
            VMEM((2, *blocks), f32),
            VMEM((6, 3, *wide), bf16),
            VMEM((6, *wide), f32),
            VMEM((2, 4, *wide), bf16),
            VMEM((2, *wide), bf16),
            VMEM((2, PIECE, D), bf16),
        )

    def sums(self, ACC, CS, OWN, XS, O2, ZS, F, FD):
        self.ACC, self.CS, self.OWN, self.XS, self.O2, self.ZS, self.F, self.FD = ACC, CS, OWN, XS, O2, ZS, F, FD

    def free(self, k, to):
        pl.semaphore_signal(self.cred.at[k], inc=1, device_id=to, device_id_type=MESH)

    def pack(self, n, block):
        b = n % 2
        for chip in range(4):
            self.CS[b, chip] = block(2 * chip + 1 - self.core).astype(bf16)
            self.OWN[b, chip] = block(2 * chip + self.core)

        @pl.when(n >= 2)
        def _():
            pl.semaphore_wait(self.cred.at[0], 1)

        self.remote(self.CS.at[b], self.CR.at[b], self.csem.at[0, b], self.csem.at[1, b], self.to(self.partner))

    def pack_gate(self, n):
        self.pack(n, lambda s: self.ACC[s])

    def downs(self, acc, sem):
        self.acc, self.acc_sem = acc, sem
        self.load_down(0)

    def load_down(self, k):
        for b in range(3):
            for h in range(2):
                src = self.dws.at[:, pl.ds(pl.multiple_of(k * PIECE + h * HALF, HALF), HALF), pl.ds(b * C, C)]
                local(src, self.ACC.at[:, pl.ds(b * HALF, HALF), pl.ds(h * C, C)], self.acc_sem).start()

    def pack_down1(self, n):
        self.done(self.ACC, self.acc_sem)
        self.pack_gate(n)
        pl.when(n < PER - 1)(lambda: self.load_down(n - NC + 1))

    def pack_down0(self, n):
        k = (n - PER) // 2

        def block(s):
            rows = []
            for b in range(3):
                sides = [self.acc[pl.ds(pl.multiple_of(s * C + k * PIECE + h * HALF, HALF), HALF), pl.ds(b * C, C)] for h in range(2)]
                rows.append(jnp.concatenate(sides, 1))
            return jnp.concatenate(rows)

        self.pack(n, block)

    def plane(self, n):
        b, xb = n % 2, n % 6
        for side, ref in enumerate((self.CS, self.CR)):
            self.done(ref.at[b], self.csem.at[side, b])

        def total(chip):
            return self.OWN[b, chip] + self.CR[b, chip].astype(f32)

        for m, chip in enumerate(self.chips):
            self.XS[xb, m] = total(chip).astype(bf16)
        self.O2[xb] = total(self.chip)
        pl.when(n + 2 < UNITS)(lambda: self.free(0, self.to(self.partner)))

        @pl.when(n >= 6)
        def _():
            for m in OTHERS:
                pl.semaphore_wait(self.cred.at[m], 1)

        for m, s in enumerate(self.planes):
            self.remote(self.XS.at[xb, m], self.XR.at[xb, m], self.xsem.at[0, xb], self.xsem.at[1, xb], self.to(s))

    def line(self, n, k, total):
        zb = n % 4
        self.ZS[k, zb] = total.astype(bf16)

        @pl.when(n >= 4)
        def _():
            pl.semaphore_wait(self.cred.at[4 + k], 1)

        self.remote(self.ZS.at[k, zb], self.ZR.at[k, zb], self.zsem.at[k, 0, zb], self.zsem.at[k, 1, zb], self.to(z=self.lines[k]))

    def line_sum(self, n, k):
        zb = n % 4
        for side, ref in enumerate((self.ZS, self.ZR)):
            self.done(ref.at[k, zb], self.zsem.at[k, side, zb])
        total = self.ZS[k, zb].astype(f32) + self.ZR[k, zb].astype(f32)
        pl.when(n + 4 < UNITS)(lambda: self.free(4 + k, self.to(z=self.lines[k])))
        return total

    def line1(self, n):
        xb = n % 6
        for side, ref in enumerate((self.XS, self.XR)):
            self.done(ref.at[xb], self.xsem.at[side, xb])
        total = self.O2[xb] + (self.XR[xb, 0].astype(f32) + self.XR[xb, 1].astype(f32) + self.XR[xb, 2].astype(f32))

        @pl.when(n + 6 < UNITS)
        def _():
            for m, s in zip(OTHERS, self.planes):
                self.free(m, self.to(s))

        self.line(n, 0, total)

    def line2(self, n):
        self.line(n, 1, self.line_sum(n, 0))

    def finish(self, n):
        total = self.line_sum(n, 1).astype(bf16)
        pl.when(n >= 2)(lambda: self.done(self.F.at[n % 2], self.osem.at[n % 2]))
        return total

    def final_gate(self, n, layer, j):
        b = n % 2
        self.F[b] = self.finish(n)
        for side in range(2):
            place = self.og.at[side, layer, :, times(j, C)]
            local(self.F.at[b, :, pl.ds(side * C, C)], place, self.osem.at[b]).start()

    def final_down(self, n, layer, k):
        b = n % 2
        total = self.finish(n)
        for i in range(3):
            for h in range(2):
                self.FD[b, pl.ds(h * HALF, HALF), pl.ds(i * C, C)] = total[i * HALF : (i + 1) * HALF, h * C : (h + 1) * C]
        local(self.FD.at[b], self.od.at[layer, times(k, PIECE)], self.osem.at[b]).start()

    def final1(self, n):
        self.final_gate(n, 1, n)

    def step2(self, j, t):
        @pl.when(t == 0)
        def _():
            @pl.when(j == 0)
            def _():
                self.third(LAST - 1)
                for u in range(PER, LAST):
                    self.whole(u)

            pl.when(j >= 1)(lambda: self.whole(LAST - 1 + j))
            pl.when(j < UNITS - LAST)(lambda: self.second(LAST + j))
            pl.when(j < UNITS - LAST - 2)(lambda: self.first(LAST + 2 + j))

        @pl.when(t == 1)
        def _():
            pl.when(j < UNITS - LAST)(lambda: self.third(LAST + j))
            for back, stage in enumerate((self.plane, self.line1, self.line2, self.final1), 1):
                pl.when(j >= back)(functools.partial(stage, j - back))

    def end2(self, j):
        self.pack_gate(j)

    def step3(self, t):
        pl.when(t <= 3)(lambda: self.final1(4 + t))
        pl.when(t >= 6)(lambda: self.final_down(2 + t, 1, t - 6))
        pl.when(t <= 2)(lambda: self.line2(5 + t))
        pl.when(t >= 4)(lambda: self.line2(4 + t))
        pl.when(t <= 1)(lambda: self.line1(6 + t))
        pl.when((t >= 3) & (t <= 6))(lambda: self.line1(5 + t))
        pl.when(t <= 4)(lambda: self.plane(7 + t))
        pl.when(t <= 3)(lambda: self.pack_down1(8 + t))

    def step4(self, it):
        pl.when(it <= 1)(lambda: self.final_down(PER - 2 + it, 1, 2 + it))
        pl.when((it == 11) | (it == 14))(lambda: self.final_down(PER + (it - 11) // 3 * 2, 0, (it - 11) // 3))
        pl.when(it == 13)(lambda: self.final_gate(PER + 1, 0, 0))
        for start, stage in ((8, self.line2), (6, self.line1)):
            @pl.when((it >= start) & ((it - start) % 3 != 1))
            def _():
                stage(PER + (2 * (it - start) + 1) // 3)

        pl.when((it >= 2) & (it <= 9))(lambda: self.plane(PER + it - 2))
        pl.when((it >= 11) & (it % 2 == 1))(lambda: self.plane(PER + NC + (it - 11) // 2))
        pl.when((it <= 7) & (it % 2 == 1))(lambda: self.pack_down0(PER + it - 1))
        pl.when((it >= 2) & (it <= 8) & (it % 2 == 0))(lambda: self.pack_gate(PER + it - 1))
        pl.when((it >= 10) & (it % 2 == 0))(lambda: self.pack_gate(PER + 3 + it // 2))

    def step5(self, t):
        pl.when((t == 1) | (t == 3))(lambda: self.final_down(PER + 3 + t, 0, (t + 3) // 2))
        pl.when((t == 0) | (t == 2))(lambda: self.final_gate(PER + 3 + t, 0, t // 2 + 1))
        pl.when(t >= 4)(lambda: self.final_gate(PER + 3 + t, 0, t - 1))
        pl.when(t <= 6)(lambda: self.line2(PER + 5 + t))
        pl.when(t <= 4)(lambda: self.line1(PER + 7 + t))
        pl.when(t == 1)(lambda: self.plane(UNITS - 1))
        pl.when(t == 0)(lambda: self.pack_gate(UNITS - 1))

    def close(self):
        self.final_gate(UNITS - 1, 0, NC - 1)
        for b in range(2):
            self.done(self.F.at[b], self.osem.at[b])
        for u in range(UNITS):
            self.done(self.unit(u, pl.ds(0, 3), 0), self.wsem.at[1, u])
            self.done(self.unit(u, slice(None), 0), self.wsem.at[5, u])


def whole(x, dy, wg, wu, wd, dx, og, od, gus, ps, dgus, h1s, a0s, dws, A, DY, WGU, WD, CR, XR, ZR, lsem, wsem, csem, xsem, zsem, osem, cred):
    links = Links(wg, wu, wd, og, od, dws, WGU, WD, CR, XR, ZR, wsem, csem, xsem, zsem, osem, cred)
    kernel(x, dy, wg, wu, wd, dx, og, od, gus, ps, dgus, h1s, a0s, dws, A, DY, WGU, WD, lsem, links)


def solution(mesh):
    def call(x, dy, wg, wu, wd):
        anywhere = pl.BlockSpec(memory_space=pl.ANY)
        S, V, M = jax.ShapeDtypeStruct, VMEM, SEM
        flops = 17 * 2 * N * D * FF
        out = pl.pallas_call(
            whole,
            in_specs=[anywhere] * 5,
            out_specs=[anywhere] * 9,
            out_shape=[
                S((N, D), bf16),
                S((2, 2, ROWS, FF), bf16),
                S((2, C, D), bf16),
                S((NC, N, WIDE), f32),
                S((N, FF), bf16),
                S((N, BOTH), bf16),
                S((N, D), bf16),
                S((N, D), bf16),
                S((NC, C, D), f32),
            ],
            scratch_shapes=[
                V((N, D), bf16),
                V((N, D), bf16),
                V((2, 4, 2, ROWS, BOTH), bf16),
                V((2, 4, 2, C, D), bf16),
                V((2, 4, ROWS, WIDE), bf16),
                V((6, 3, ROWS, WIDE), bf16),
                V((2, 4, ROWS, WIDE), bf16),
                PAIR,
                M((6, UNITS)),
                M((2, 2)),
                M((2, 6)),
                M((2, 2, 4)),
                PAIR,
                pltpu.SemaphoreType.REGULAR((6,)),
            ],
            compiler_params=pltpu.CompilerParams(vmem_limit_bytes=67_000_000, collective_id=0, has_side_effects=True),
            cost_estimate=pl.CostEstimate(flops=flops, bytes_accessed=400_000_000, transcendentals=0),
            name="stack",
        )(x, dy, wg, wu, wd)
        return out[:3]

    def step(x, dy, wg, wu, wd):
        dx, sides, down = call(x[0], dy[0], wg, wu, wd)
        return dx[None], sides[0], sides[1], down

    states, cut = P(("rep", "r", "s"), None, None), P(None, "s", None)
    return jax.shard_map(
        step,
        mesh=mesh,
        in_specs=(states, states) + (cut,) * 3,
        out_specs=(states,) + (P("rep", "s", None),) * 3,
        check_vma=False,
    )
```

time: 332 us -> 314 us (0.946)
  Pallas kernels: 322 us -> 304 us
    pallas_call x1, Pallas kernels: 322 us -> 304 us  [call(): pl.pallas_call(whole, in_specs=[anywhere] * 5, out_specs=[anywhere] * 9,...]
where the time goes in v2:
time: 314 us
  Pallas kernels  304 us (97%)
  local copies, waits for them, and re-layouts  9.54 us (3%)
    pallas_call x1, Pallas kernels, call(): pl.pallas_call(whole, in_specs=[anywhere] * 5, out_specs=[anywhere] * 9,...  304 us
    unnamed x4, local copies, waits for them, and re-layouts  6.85 us

profile of v2, /device:TPU:0, one launch (start us, length us, event | category | flops | bytes accessed | tf_op | source)
XLA Modules:
  0.0 313.9 jit_solution(8573918471422597881)
XLA Ops:
  0.6 303.7 %stack.1 = (bf16[4096,768]{1,0:T(8,128)(2,1)}, bf16[2,2,96,2048]{3,2,1,0:T(8,128)(2,1)}, bf16[2,256,768]{2,1,0:T(8,128)(2,1)}, f32[8,4096,512]{2,1,0:T(8,128)}, ...) custom-call(bf16[4096,768]{1,0:T(8,128)(2,1)} %bitcast.8, ...), custom_call_target="tpu_custom_call" | custom-call | flops 219043332096 | bytes 400000000 | tf_op jit(solution)/shard_map/stack/pallas_call | solution.py:671
  304.4 2.7 slice_bitcast_fusion
  307.1 0.0 copy-start
  307.1 6.0 %copy.11 = bf16[1,4096,768]{2,1,0:T(8,128)(2,1)} copy(bf16[1,4096,768]{2,1,0:T(8,128)(2,1)} %bitcast.7) | data formatting | bytes 12582912
  313.0 0.0 copy-done
  313.0 0.9 copy.12
Async XLA Ops:
  307.1 6.0 %copy-start = (bf16[2,256,768]{2,1,0:T(8,128)(2,1)S(1)}, bf16[2,256,768]{2,1,0:T(8,128)(2,1)}, u32[]{:S(2)}) copy-start(bf16[2,256,768]{2,1,0:T(8,128)(2,1)} %get-tuple-element.19) | copy-start | bytes 2359300

commit v3 on v2

--- a/solution.py
+++ b/solution.py
@@ -17,8 +17,9 @@
 DOWNS = (NC, PER + 1)
 LAST = 17
 OTHERS = (1, 2, 3)
+SENT, CAME, LINE = 5, 6, 3
 T0, T1, T2, T3, T4, T5 = FF, WIDE, FF, WIDE, FF, WIDE
-S0, S1, S2, S3, S4, S5 = 4, 2, 4, 2, 4, 2
+S0, S1, S2, S3, S4 = 4, 2, 4, 2, 4
 M3 = 4
 f32, bf16 = jnp.float32, jnp.bfloat16
 NN = (((1,), (0,)), ((), ()))
@@ -108,11 +109,11 @@
     return jnp.where(t == 0, 0.0, ref) + term
 
 
-def kernel(x, dy, wg, wu, wd, dx, og, od, gus, ps, dgus, h1s, a0s, dws, A, DY, WGU, WD, lsem, go):
+def kernel(x, dy, wg, wu, wd, dx, og, ou, od, gus, ps, dgus, h1s, a0s, dws, A, DY, WGU, WD, lsem, go):
     x_in, dy_in = local(x, A, lsem.at[0]), local(dy, DY, lsem.at[1])
     a_out, a_in = local(A, a0s, lsem.at[0]), local(a0s, A, lsem.at[0])
+    go.own(0)
     x_in.start()
-    dy_in.start()
     go.open()
     x_in.wait()
 
@@ -122,21 +123,22 @@
 
     a_out.start()
     go.weights_first()
-
-    def forward(hid, stg, stx, sth, sp, ss, sx, sh):
-        x_tile = states_in(stx, sx)
+    dy_in.start()
+
+    def forward(hid, stg, st, sp, ss, sx, sh):
+        x_tile = states_in(st, sx)
         arrive_later = x_tile(0)
         for c in arrive_later:
             c.start()
         kept = hidden0(hid, stg, ss)
         a_out.wait()
         local(hid, ps, sp).start()
-        states1(hid, stx, sth, x_tile, sh)
+        states1(hid, st, x_tile, sh)
         arrive(kept)
         local(hid, ps, sp).wait()
 
-    def states_in(stx, sx):
-        return lambda t: [local(x.at[times(t, T1)], stx.at[t % 2], sx.at[t % 2])]
+    def states_in(st, sx):
+        return lambda t: [local(x.at[times(t, T1)], st.at[t % 3], sx.at[t % 3])]
 
     def hidden0(hid, stg, ss):
         B, nt = T0 // S0, N // T0
@@ -159,30 +161,29 @@
         loop(NC * nt, tile)
         return map(leave, range(2))
 
-    def states1(hid, stx, sth, come, ss):
+    def states1(hid, st, come, ss):
         B, nt = T1 // S1, N // T1
 
         def leave(t):
-            return local(sth.at[t % 2], h1s.at[times(t, T1)], ss.at[t % 2])
+            return local(st.at[t % 3], h1s.at[times(t, T1)], ss.at[t % 3])
 
         def tile(t):
-            slot = t % 2
+            slot = t % 3
+            pl.when(t >= 2)(lambda: leave(t - 2).wait())
             fetch(t, nt, come, True)
-            again(t, leave(t))
             arrive(come(t))
             go.step1(t)
             for k in range(S1):
                 m = dot(hid[pl.ds(t * T1 + k * B, B), :], WD[0].reshape(FF, D)).astype(bf16)
-                h = (stx[slot, pl.ds(k * B, B)].astype(f32) + m.astype(f32)).astype(bf16)
-                sth[slot, pl.ds(k * B, B)] = h
+                h = (st[slot, pl.ds(k * B, B)].astype(f32) + m.astype(f32)).astype(bf16)
+                st[slot, pl.ds(k * B, B)] = h
                 A[pl.ds(t * T1 + k * B, B), :] = normed(h)
             leave(t).start()
 
         loop(nt, tile)
-        arrive(map(leave, range(2)))
-
-    tiles1 = VMEM((2, T1, D), bf16)
-    pl.run_scoped(forward, VMEM((N, FF), bf16), VMEM((2, T0, WIDE), f32), tiles1, tiles1, SEM, PAIR, PAIR, PAIR)
+        arrive(map(leave, range(nt - 2, nt)))
+
+    pl.run_scoped(forward, VMEM((N, FF), bf16), VMEM((2, T0, WIDE), f32), VMEM((3, T1, D), bf16), SEM, PAIR, SEM((3,)), SEM((3,)))
 
     def backward(ACC, *sums):
         go.sums(ACC, *sums)
@@ -212,7 +213,7 @@
                     stg[slot, pl.ds(k * B, B)] = by_gu
                     dgu.append(by_gu)
                     p.append(hidden.astype(bf16))
-                ACC[...] = added(t, ACC[...], dot(A[r, :], jnp.concatenate(dgu), TN).reshape(ACC.shape))
+                ACC[here] = added(t, ACC[here], dot(A[r, :], jnp.concatenate(dgu), TN).reshape(NC, ROWS, WIDE))
                 acc[here] = added(t, acc[here], dot(jnp.concatenate(p), DY[r, :], TN))
                 leave(it).start()
 
@@ -281,7 +282,7 @@
                         by_gu, _ = back(gu[:, :C], gu[:, C:], dp)
                         stg[slot, pl.ds(k * B, B)] = by_gu
                         dgu.append(by_gu)
-                    ACC[...] = added(t, ACC[...], dot(A[times(t, T4), :], jnp.concatenate(dgu), TN).reshape(ACC.shape))
+                    ACC[j % 2] = added(t, ACC[j % 2], dot(A[times(t, T4), :], jnp.concatenate(dgu), TN).reshape(NC, ROWS, WIDE))
                     leave(it).start()
 
                 loop(NC * nt, tile)
@@ -292,39 +293,53 @@
 
         pl.run_scoped(first_layer, VMEM((FF, D), f32), SEM)
 
-        def last(sg, sh, so, ss, *sems):
-            B, nt = T5 // S5, N // T5
+        def last(sg, sh, so, pending, ss, *sems):
+            B, nt = T5 // 2, N // T5
 
             def come(t):
-                pairs = (dgus, sg), (x, sh)
-                return [local(src.at[times(t, T5)], dst.at[t % 2], sem.at[t % 2]) for (src, dst), sem in zip(pairs, sems)]
+                pairs = (dgus, sg, 2), (x, sh, 3)
+                return [local(src.at[times(t, T5)], dst.at[t % k], sem.at[t % k]) for (src, dst, k), sem in zip(pairs, sems)]
 
             def leave(t):
-                return local(so.at[t % 2], dx.at[times(t, T5)], ss.at[t % 2])
+                return local(so.at[t % 3], dx.at[times(t, T5)], ss.at[t % 3])
+
+            def finish(slot, t, part, da):
+                so[slot, times(part, B)] = norm_back(sh[slot, times(part, B)], da, DY[pl.ds(t * T5 + part * B, B), :])
 
             def tile(t):
-                slot = t % 2
                 fetch(t, nt, come)
-                again(t, leave(t))
+                pl.when(t >= 3)(leave(t).wait)
                 go.step5(t)
                 arrive(come(t))
-                for k in range(S5):
-                    da = dot(sg[slot, pl.ds(k * B, B), :], gates(WGU, 0), NT)
-                    so[slot, pl.ds(k * B, B)] = norm_back(sh[slot, pl.ds(k * B, B)], da, DY[pl.ds(t * T5 + k * B, B), :])
-                leave(t).start()
+                finish((t + 2) % 3, (t + nt - 1) % nt, 1, pending[...])
+                by_a = [dot(sg[t % 2, times(k, B), :], gates(WGU, 0), NT) for k in range(2)]
+                finish(t % 3, t, 0, by_a[0])
+                pending[...] = by_a[1]
+                pl.when(t >= 1)(lambda: leave(t - 1).start())
 
             loop(nt, tile)
-            arrive(map(leave, range(2)))
-
-        pl.run_scoped(last, VMEM((2, T5, BOTH), bf16), VMEM((2, T5, D), bf16), VMEM((2, T5, D), bf16), PAIR, PAIR, PAIR)
+            finish((nt - 1) % 3, nt - 1, 1, pending[...])
+            leave(nt - 1).start()
+            arrive(map(leave, range(nt - 3, nt)))
+
+        pl.run_scoped(
+            last,
+            VMEM((2, T5, BOTH), bf16),
+            VMEM((3, T5, D), bf16),
+            VMEM((3, T5, D), bf16),
+            VMEM((T5 // 2, D), f32),
+            SEM((3,)),
+            PAIR,
+            SEM((3,)),
+        )
         go.close()
 
-    pl.run_scoped(backward, VMEM((NC, ROWS, WIDE), f32), *go.scratch())
+    pl.run_scoped(backward, VMEM((2, NC, ROWS, WIDE), f32), *go.scratch())
 
 
 class Links:
-    def __init__(self, wg, wu, wd, og, od, dws, WGU, WD, CR, XR, ZR, wsem, csem, xsem, zsem, osem, cred):
-        self.wg, self.wu, self.wd, self.og, self.od, self.dws, self.WGU, self.WD = wg, wu, wd, og, od, dws, WGU, WD
+    def __init__(self, wg, wu, wd, og, ou, od, dws, WGU, WD, CR, XR, ZR, wsem, csem, xsem, zsem, osem, cred):
+        self.wg, self.wu, self.wd, self.outs, self.od, self.dws, self.WGU, self.WD = wg, wu, wd, (og, ou), od, dws, WGU, WD
         self.CR, self.XR, self.ZR = CR, XR, ZR
         self.wsem, self.csem, self.xsem, self.zsem, self.osem, self.cred = wsem, csem, xsem, zsem, osem, cred
         s, z = lax.axis_index("s"), lax.axis_index("r")
@@ -405,7 +420,6 @@
                 self.third(u)
 
     def open(self):
-        self.own(0)
         self.own(1)
         barrier = pltpu.get_barrier_semaphore()
         peers = [self.to(self.partner)] + [self.to(s) for s in self.planes] + [self.to(z=z) for z in self.lines]
@@ -459,16 +473,15 @@
         blocks, wide = (4, ROWS, WIDE), (ROWS, WIDE)
         return (
             VMEM((2, *blocks), bf16),
-            VMEM((2, *blocks), f32),
-            VMEM((6, 3, *wide), bf16),
-            VMEM((6, *wide), f32),
-            VMEM((2, 4, *wide), bf16),
+            VMEM((SENT, 3, *wide), bf16),
+            VMEM((CAME, *wide), f32),
+            VMEM((2, LINE, *wide), bf16),
             VMEM((2, *wide), bf16),
             VMEM((2, PIECE, D), bf16),
         )
 
-    def sums(self, ACC, CS, OWN, XS, O2, ZS, F, FD):
-        self.ACC, self.CS, self.OWN, self.XS, self.O2, self.ZS, self.F, self.FD = ACC, CS, OWN, XS, O2, ZS, F, FD
+    def sums(self, ACC, CS, XS, O2, ZS, F, FD):
+        self.ACC, self.CS, self.XS, self.O2, self.ZS, self.F, self.FD = ACC, CS, XS, O2, ZS, F, FD
 
     def free(self, k, to):
         pl.semaphore_signal(self.cred.at[k], inc=1, device_id=to, device_id_type=MESH)
@@ -477,7 +490,6 @@
         b = n % 2
         for chip in range(4):
             self.CS[b, chip] = block(2 * chip + 1 - self.core).astype(bf16)
-            self.OWN[b, chip] = block(2 * chip + self.core)
 
         @pl.when(n >= 2)
         def _():
@@ -485,8 +497,11 @@
 
         self.remote(self.CS.at[b], self.CR.at[b], self.csem.at[0, b], self.csem.at[1, b], self.to(self.partner))
 
-    def pack_gate(self, n):
-        self.pack(n, lambda s: self.ACC[s])
+    def pack_gate(self, n, slot):
+        self.pack(n, lambda s: self.ACC[slot, s])
+
+    def plane_gate(self, n, slot):
+        self.plane(n, lambda s: self.ACC[slot, s])
 
     def downs(self, acc, sem):
         self.acc, self.acc_sem = acc, sem
@@ -496,16 +511,14 @@
         for b in range(3):
             for h in range(2):
                 src = self.dws.at[:, pl.ds(pl.multiple_of(k * PIECE + h * HALF, HALF), HALF), pl.ds(b * C, C)]
-                local(src, self.ACC.at[:, pl.ds(b * HALF, HALF), pl.ds(h * C, C)], self.acc_sem).start()
+                local(src, self.ACC.at[k % 2, :, pl.ds(b * HALF, HALF), pl.ds(h * C, C)], self.acc_sem).start()
 
     def pack_down1(self, n):
-        self.done(self.ACC, self.acc_sem)
-        self.pack_gate(n)
+        self.done(self.ACC.at[n % 2], self.acc_sem)
+        self.pack_gate(n, n % 2)
         pl.when(n < PER - 1)(lambda: self.load_down(n - NC + 1))
 
-    def pack_down0(self, n):
-        k = (n - PER) // 2
-
+    def down0(self, k):
         def block(s):
             rows = []
             for b in range(3):
@@ -513,54 +526,54 @@
                 rows.append(jnp.concatenate(sides, 1))
             return jnp.concatenate(rows)
 
-        self.pack(n, block)
-
-    def plane(self, n):
-        b, xb = n % 2, n % 6
+        return block
+
+    def plane(self, n, block):
+        b, xs, xb = n % 2, n % SENT, n % CAME
         for side, ref in enumerate((self.CS, self.CR)):
             self.done(ref.at[b], self.csem.at[side, b])
 
         def total(chip):
-            return self.OWN[b, chip] + self.CR[b, chip].astype(f32)
+            return block(2 * chip + self.core) + self.CR[b, chip].astype(f32)
 
         for m, chip in enumerate(self.chips):
-            self.XS[xb, m] = total(chip).astype(bf16)
+            self.XS[xs, m] = total(chip).astype(bf16)
         self.O2[xb] = total(self.chip)
         pl.when(n + 2 < UNITS)(lambda: self.free(0, self.to(self.partner)))
 
-        @pl.when(n >= 6)
+        @pl.when(n >= CAME)
         def _():
             for m in OTHERS:
                 pl.semaphore_wait(self.cred.at[m], 1)
 
         for m, s in enumerate(self.planes):
-            self.remote(self.XS.at[xb, m], self.XR.at[xb, m], self.xsem.at[0, xb], self.xsem.at[1, xb], self.to(s))
+            self.remote(self.XS.at[xs, m], self.XR.at[xb, m], self.xsem.at[0, xs], self.xsem.at[1, xb], self.to(s))
 
     def line(self, n, k, total):
-        zb = n % 4
+        zb = n % LINE
         self.ZS[k, zb] = total.astype(bf16)
 
-        @pl.when(n >= 4)
+        @pl.when(n >= LINE)
         def _():
             pl.semaphore_wait(self.cred.at[4 + k], 1)
 
         self.remote(self.ZS.at[k, zb], self.ZR.at[k, zb], self.zsem.at[k, 0, zb], self.zsem.at[k, 1, zb], self.to(z=self.lines[k]))
 
     def line_sum(self, n, k):
-        zb = n % 4
+        zb = n % LINE
         for side, ref in enumerate((self.ZS, self.ZR)):
             self.done(ref.at[k, zb], self.zsem.at[k, side, zb])
         total = self.ZS[k, zb].astype(f32) + self.ZR[k, zb].astype(f32)
-        pl.when(n + 4 < UNITS)(lambda: self.free(4 + k, self.to(z=self.lines[k])))
+        pl.when(n + LINE < UNITS)(lambda: self.free(4 + k, self.to(z=self.lines[k])))
         return total
 
     def line1(self, n):
-        xb = n % 6
-        for side, ref in enumerate((self.XS, self.XR)):
-            self.done(ref.at[xb], self.xsem.at[side, xb])
+        xs, xb = n % SENT, n % CAME
+        self.done(self.XS.at[xs], self.xsem.at[0, xs])
+        self.done(self.XR.at[xb], self.xsem.at[1, xb])
         total = self.O2[xb] + (self.XR[xb, 0].astype(f32) + self.XR[xb, 1].astype(f32) + self.XR[xb, 2].astype(f32))
 
-        @pl.when(n + 6 < UNITS)
+        @pl.when(n + CAME < UNITS)
         def _():
             for m, s in zip(OTHERS, self.planes):
                 self.free(m, self.to(s))
@@ -578,9 +591,8 @@
     def final_gate(self, n, layer, j):
         b = n % 2
         self.F[b] = self.finish(n)
-        for side in range(2):
-            place = self.og.at[side, layer, :, times(j, C)]
-            local(self.F.at[b, :, pl.ds(side * C, C)], place, self.osem.at[b]).start()
+        for side, out in enumerate(self.outs):
+            local(self.F.at[b, :, pl.ds(side * C, C)], out.at[layer, :, times(j, C)], self.osem.at[b]).start()
 
     def final_down(self, n, layer, k):
         b = n % 2
@@ -609,11 +621,12 @@
         @pl.when(t == 1)
         def _():
             pl.when(j < UNITS - LAST)(lambda: self.third(LAST + j))
-            for back, stage in enumerate((self.plane, self.line1, self.line2, self.final1), 1):
+            pl.when(j >= 1)(lambda: self.plane_gate(j - 1, (j - 1) % 2))
+            for back, stage in enumerate((self.line1, self.line2, self.final1), 2):
                 pl.when(j >= back)(functools.partial(stage, j - back))
 
     def end2(self, j):
-        self.pack_gate(j)
+        self.pack_gate(j, j % 2)
 
     def step3(self, t):
         pl.when(t <= 3)(lambda: self.final1(4 + t))
@@ -622,7 +635,7 @@
         pl.when(t >= 4)(lambda: self.line2(4 + t))
         pl.when(t <= 1)(lambda: self.line1(6 + t))
         pl.when((t >= 3) & (t <= 6))(lambda: self.line1(5 + t))
-        pl.when(t <= 4)(lambda: self.plane(7 + t))
+        pl.when(t <= 4)(lambda: self.plane_gate(7 + t, (7 + t) % 2))
         pl.when(t <= 3)(lambda: self.pack_down1(8 + t))
 
     def step4(self, it):
@@ -634,11 +647,23 @@
             def _():
                 stage(PER + (2 * (it - start) + 1) // 3)
 
-        pl.when((it >= 2) & (it <= 9))(lambda: self.plane(PER + it - 2))
-        pl.when((it >= 11) & (it % 2 == 1))(lambda: self.plane(PER + NC + (it - 11) // 2))
-        pl.when((it <= 7) & (it % 2 == 1))(lambda: self.pack_down0(PER + it - 1))
-        pl.when((it >= 2) & (it <= 8) & (it % 2 == 0))(lambda: self.pack_gate(PER + it - 1))
-        pl.when((it >= 10) & (it % 2 == 0))(lambda: self.pack_gate(PER + 3 + it // 2))
+        @pl.when(it % 2 == 0)
+        def _():
+            j = it // 2 - 1
+
+            @pl.when((j >= 0) & (j <= 3))
+            def _():
+                self.plane(PER + it - 2, self.down0(j))
+                self.pack_gate(PER + it - 1, j % 2)
+
+            pl.when(j >= 4)(lambda: self.pack_gate(2 * NC + j, j % 2))
+
+        @pl.when(it % 2 == 1)
+        def _():
+            k = it // 2
+            pl.when((k >= 1) & (k <= 4))(lambda: self.plane_gate(PER + it - 2, (k - 1) % 2))
+            pl.when(k >= 5)(lambda: self.plane_gate(2 * NC + k - 1, (k - 1) % 2))
+            pl.when(k <= 3)(lambda: self.pack(PER + it - 1, self.down0(k)))
 
     def step5(self, t):
         pl.when((t == 1) | (t == 3))(lambda: self.final_down(PER + 3 + t, 0, (t + 3) // 2))
@@ -646,8 +671,8 @@
         pl.when(t >= 4)(lambda: self.final_gate(PER + 3 + t, 0, t - 1))
         pl.when(t <= 6)(lambda: self.line2(PER + 5 + t))
         pl.when(t <= 4)(lambda: self.line1(PER + 7 + t))
-        pl.when(t == 1)(lambda: self.plane(UNITS - 1))
-        pl.when(t == 0)(lambda: self.pack_gate(UNITS - 1))
+        pl.when(t == 1)(lambda: self.plane_gate(UNITS - 1, 1))
+        pl.when(t == 0)(lambda: self.pack_gate(UNITS - 1, 1))
 
     def close(self):
         self.final_gate(UNITS - 1, 0, NC - 1)
@@ -658,9 +683,9 @@
             self.done(self.unit(u, slice(None), 0), self.wsem.at[5, u])
 
 
-def whole(x, dy, wg, wu, wd, dx, og, od, gus, ps, dgus, h1s, a0s, dws, A, DY, WGU, WD, CR, XR, ZR, lsem, wsem, csem, xsem, zsem, osem, cred):
-    links = Links(wg, wu, wd, og, od, dws, WGU, WD, CR, XR, ZR, wsem, csem, xsem, zsem, osem, cred)
-    kernel(x, dy, wg, wu, wd, dx, og, od, gus, ps, dgus, h1s, a0s, dws, A, DY, WGU, WD, lsem, links)
+def whole(x, dy, wg, wu, wd, dx, og, ou, od, gus, ps, dgus, h1s, a0s, dws, A, DY, WGU, WD, CR, XR, ZR, lsem, wsem, csem, xsem, zsem, osem, cred):
+    links = Links(wg, wu, wd, og, ou, od, dws, WGU, WD, CR, XR, ZR, wsem, csem, xsem, zsem, osem, cred)
+    kernel(x, dy, wg, wu, wd, dx, og, ou, od, gus, ps, dgus, h1s, a0s, dws, A, DY, WGU, WD, lsem, links)
 
 
 def solution(mesh):
@@ -671,10 +696,11 @@
         out = pl.pallas_call(
             whole,
             in_specs=[anywhere] * 5,
-            out_specs=[anywhere] * 9,
+            out_specs=[anywhere] * 10,
             out_shape=[
                 S((N, D), bf16),
-                S((2, 2, ROWS, FF), bf16),
+                S((2, ROWS, FF), bf16),
+                S((2, ROWS, FF), bf16),
                 S((2, C, D), bf16),
                 S((NC, N, WIDE), f32),
                 S((N, FF), bf16),
@@ -689,13 +715,13 @@
                 V((2, 4, 2, ROWS, BOTH), bf16),
                 V((2, 4, 2, C, D), bf16),
                 V((2, 4, ROWS, WIDE), bf16),
-                V((6, 3, ROWS, WIDE), bf16),
-                V((2, 4, ROWS, WIDE), bf16),
+                V((CAME, 3, ROWS, WIDE), bf16),
+                V((2, LINE, ROWS, WIDE), bf16),
                 PAIR,
                 M((6, UNITS)),
                 M((2, 2)),
-                M((2, 6)),
-                M((2, 2, 4)),
+                M((2, CAME)),
+                M((2, 2, LINE)),
                 PAIR,
                 pltpu.SemaphoreType.REGULAR((6,)),
             ],
@@ -703,11 +729,11 @@
             cost_estimate=pl.CostEstimate(flops=flops, bytes_accessed=400_000_000, transcendentals=0),
             name="stack",
         )(x, dy, wg, wu, wd)
-        return out[:3]
+        return out[:4]
 
     def step(x, dy, wg, wu, wd):
-        dx, sides, down = call(x[0], dy[0], wg, wu, wd)
-        return dx[None], sides[0], sides[1], down
+        dx, *by_weights = call(x[0], dy[0], wg, wu, wd)
+        return dx[None], *by_weights
 
     states, cut = P(("rep", "r", "s"), None, None), P(None, "s", None)
     return jax.shard_map(

time: 314 us -> 312 us (level)
    unnamed x4 -> x10, local copies, waits for them, and re-layouts: 6.85 us -> 8.69 us
where the time goes in v3:
time: 312 us
  Pallas kernels  303 us (97%)
  local copies, waits for them, and re-layouts  8.69 us (3%)
    pallas_call x1, Pallas kernels, call(): pl.pallas_call(whole, in_specs=[anywhere] * 5, out_specs=[anywhere] * 10,...  303 us
    unnamed x10, local copies, waits for them, and re-layouts  8.69 us

profile of v3, /device:TPU:0, one launch (start us, length us, event | category | flops | bytes accessed | tf_op | source)
XLA Modules:
  0.0 312.2 jit_solution(2333524589222584776)
XLA Ops:
  0.6 302.9 %stack.1 = (bf16[4096,768]{1,0:T(8,128)(2,1)}, bf16[2,96,2048]{2,1,0:T(8,128)(2,1)}, bf16[2,96,2048]{2,1,0:T(8,128)(2,1)}, bf16[2,256,768]{2,1,0:T(8,128)(2,1)},...) custom-call(bf16[4096,768]{1,0:T(8,128)(2,1)} %bitcast.4, ...), custom_call_target="tpu_custom_call" | custom-call | flops 219043332096 | bytes 400000000 | tf_op jit(solution)/shard_map/stack/pallas_call | solution.py:696
  303.5 0.0 copy-start.2
  303.5 0.0 copy-start.1
  303.5 0.0 copy-start
  303.6 6.0 %copy.13 = bf16[1,4096,768]{2,1,0:T(8,128)(2,1)} copy(bf16[1,4096,768]{2,1,0:T(8,128)(2,1)} %bitcast.3) | data formatting | bytes 12582912
  309.6 0.0 copy-done.2
  309.6 0.9 copy.14
  310.5 0.0 copy-done.1
  310.5 0.9 copy.15
  311.4 0.0 copy-done
  311.4 0.9 copy.16
Async XLA Ops:
  303.5 6.1 %copy-start.2 = (bf16[2,96,2048]{2,1,0:T(8,128)(2,1)S(1)}, bf16[2,96,2048]{2,1,0:T(8,128)(2,1)}, u32[]{:S(2)}) copy-start(bf16[2,96,2048]{2,1,0:T(8,128)(2,1)} %get-tuple-element.17) | copy-start | bytes 2359300
  303.5 6.9 %copy-start.1 = (bf16[2,96,2048]{2,1,0:T(8,128)(2,1)S(1)}, bf16[2,96,2048]{2,1,0:T(8,128)(2,1)}, u32[]{:S(2)}) copy-start(bf16[2,96,2048]{2,1,0:T(8,128)(2,1)} %get-tuple-element.18) | copy-start | bytes 2359300
  303.5 7.8 %copy-start = (bf16[2,256,768]{2,1,0:T(8,128)(2,1)S(1)}, bf16[2,256,768]{2,1,0:T(8,128)(2,1)}, u32[]{:S(2)}) copy-start(bf16[2,256,768]{2,1,0:T(8,128)(2,1)} %get-tuple-element.19) | copy-start | bytes 2359300

commit v4 on v3

--- a/solution.py
+++ b/solution.py
@@ -686,6 +686,20 @@
 def whole(x, dy, wg, wu, wd, dx, og, ou, od, gus, ps, dgus, h1s, a0s, dws, A, DY, WGU, WD, CR, XR, ZR, lsem, wsem, csem, xsem, zsem, osem, cred):
     links = Links(wg, wu, wd, og, ou, od, dws, WGU, WD, CR, XR, ZR, wsem, csem, xsem, zsem, osem, cred)
     kernel(x, dy, wg, wu, wd, dx, og, ou, od, gus, ps, dgus, h1s, a0s, dws, A, DY, WGU, WD, lsem, links)
+
+
+def hand_out(*refs):
+    count = len(refs) // 3
+    ins, outs, held, (come, leave) = refs[:count], refs[count : 2 * count], refs[2 * count : 3 * count], refs[3 * count :]
+    pieces = [(0, pl.ds(k * N // 4, N // 4)) for k in range(4)] + [(i, slice(None)) for i in range(1, count)]
+    arriving = [local(ins[i].at[rows], held[i].at[rows], come.at[k]) for k, (i, rows) in enumerate(pieces)]
+    leaving = [local(held[i].at[rows], outs[i].at[rows], leave.at[k]) for k, (i, rows) in enumerate(pieces)]
+    for copy in arriving:
+        copy.start()
+    for first, second in zip(arriving, leaving):
+        first.wait()
+        second.start()
+    arrive(leaving)
 
 
 def solution(mesh):
@@ -729,7 +743,16 @@
             cost_estimate=pl.CostEstimate(flops=flops, bytes_accessed=400_000_000, transcendentals=0),
             name="stack",
         )(x, dy, wg, wu, wd)
-        return out[:4]
+        kept = [S(o.shape, bf16) for o in out[:4]]
+        return pl.pallas_call(
+            hand_out,
+            in_specs=[anywhere] * 4,
+            out_specs=[anywhere] * 4,
+            out_shape=kept,
+            scratch_shapes=[V(o.shape, bf16) for o in kept] + [M((7,)), M((7,))],
+            compiler_params=pltpu.CompilerParams(vmem_limit_bytes=67_000_000),
+            name="hand_out",
+        )(*out[:4])
 
     def step(x, dy, wg, wu, wd):
         dx, *by_weights = call(x[0], dy[0], wg, wu, wd)

time: 312 us -> 311 us (level)
  local copies, waits for them, and re-layouts: 8.69 us -> 0 us
  Pallas kernels: 303 us -> 310 us
    unnamed x10 -> x0, local copies, waits for them, and re-layouts: 8.69 us -> none
    pallas_call x0 -> x1, Pallas kernels: none -> 6.87 us  [call(): pl.pallas_call(hand_out, in_specs=[anywhere] * 4, out_specs=[anywhere] *...]
where the time goes in v4:
time: 311 us
  Pallas kernels  310 us (100%)
    pallas_call x1, Pallas kernels, call(): pl.pallas_call(whole, in_specs=[anywhere] * 5, out_specs=[anywhere] * 10,...  303 us
    pallas_call x1, Pallas kernels, call(): pl.pallas_call(hand_out, in_specs=[anywhere] * 4, out_specs=[anywhere] *...  6.87 us

profile of v4, /device:TPU:0, one launch (start us, length us, event | category | flops | bytes accessed | tf_op | source)
XLA Modules:
  0.0 310.6 jit_solution(2179176343540981844)
XLA Ops:
  0.6 302.9 %stack.1 = (bf16[4096,768]{1,0:T(8,128)(2,1)}, bf16[2,96,2048]{2,1,0:T(8,128)(2,1)}, bf16[2,96,2048]{2,1,0:T(8,128)(2,1)}, bf16[2,256,768]{2,1,0:T(8,128)(2,1)},...) custom-call(bf16[4096,768]{1,0:T(8,128)(2,1)} %bitcast.3, ...), custom_call_target="tpu_custom_call" | custom-call | flops 219043332096 | bytes 400000000 | tf_op jit(solution)/shard_map/stack/pallas_call | solution.py:710
  303.6 6.9 %hand_out.1 = (bf16[4096,768]{1,0:T(8,128)(2,1)}, bf16[2,96,2048]{2,1,0:T(8,128)(2,1)}, bf16[2,96,2048]{2,1,0:T(8,128)(2,1)}, bf16[2,256,768]{2,1,0:T(8,128)(2,1)}) custom-call(bf16[4096,768]{1,0:T(8,128)(2,1)} %get-tuple-element.12.refs_0_, bf16[2,96,2048]{2,1,0:T(8,128)(2,1)} %get-tuple-element.13.refs_1_, bf16[2,96,2048]{2,1,0:T(8,128)(2,1)} %get-tuple-element.14.refs_2_, ...), custom_call_target="tpu_custom_call" | custom-call | tf_op jit(solution)/shard_map/hand_out/pallas_call | solution.py:747
